TPU v7x, 256 devices: a whole 4x4x8 slice. The times are simulated.
256 devices in a mesh: wide: 64 (over y, z_hi, x), narrow: 4 (over z_lo, core).
Axes of the slice: x: 4, y: 4, z: 8 (z_hi: 4, z_lo: 2; z = z_hi * 2 + z_lo), core: 2. Of those that a mesh axis runs over, the one named last changes fastest.
Arguments:
- value_in: float32 [128, 16, 16, 512], P('wide', None, None, 'narrow'), may hold values from -6 to 6
- payoff: float32 [128, 16, 16, 512], P('wide', None, None, 'narrow'), may hold values from -6 to 6
- diffusion: float32 [4, 128, 16, 16, 512], P(None, 'wide', None, None, 'narrow'), may hold values from 0.25 to 2
- cross_terms: float32 [6, 128, 16, 16, 512], P(None, 'wide', None, None, 'narrow'), may hold values from -0.3 to 0.3
- flags: int32 [1, 128, 16, 16, 512], P(None, 'wide', None, None, 'narrow'), may hold values 0 or 1
- cotangent: float32 [128, 16, 16, 512], P('wide', None, None, 'narrow'), may hold values from -6 to 6
Outputs:
- grad_value: float32 [128, 16, 16, 512], P('wide', None, None, 'narrow')
- grad_payoff: float32 [128, 16, 16, 512], P('wide', None, None, 'narrow')
- grad_diffusion: float32 [4, 128, 16, 16, 512], P(None, 'wide', None, None, 'narrow')
- grad_cross: float32 [6, 128, 16, 16, 512], P(None, 'wide', None, None, 'narrow')
All inputs are finite; a program needn't handle non-finite values. No bound on the sum of `flags` on one device may be relied on, other than what follows from the above.
Results may differ from a plain program's by a relative error of at most 0.00002.
Values sent between devices are 32-bit elements; how exact they have to be, the bound alone decides.
No kernel may reach another device: no remote copies, remote signals or barrier semaphores. Data moves between devices by JAX's collectives and lax.ppermute only.
A program may use at most 192 MiB of HBM per device.

v0:
```python
import jax
import jax.numpy as jnp
from jax import lax
from jax.sharding import PartitionSpec as P

STEPS = 1
SWEEPS = 2


asset_pairs = ((0, 1), (0, 2), (0, 3), (1, 2), (1, 3), (2, 3))
remote_pairs = (0, 1, 2, 4, 5)


def extended_2(cells, sides, width):
    for axis, dim in sides:
        count = lax.axis_size(axis)
        ends = count - 1
        head = lax.slice_in_dim(cells, 0, width, axis=dim)
        tail = lax.slice_in_dim(cells, cells.shape[dim] - width, cells.shape[dim], axis=dim)
        cells = jnp.concatenate(
            [
                lax.ppermute(tail, axis, [(i, (i + 1) % count) for i in range(ends)]),
                cells,
                lax.ppermute(head, axis, [((i + 1) % count, i) for i in range(ends)]),
            ],
            axis=dim,
        )
    return cells


def offset_view(padded, offsets):
    return padded[
        tuple(
            (
                slice(1 + offset, padded.shape[dimension] - 1 + offset)
                for dimension, offset in enumerate(offsets)
            )
        )
    ]


def unit_step(first, second, sign_first, sign_second):
    return tuple(
        (
            (sign_first if dimension == first else 0) + (sign_second if dimension == second else 0)
            for dimension in range(4)
        )
    )


def neighbours(padded, first):
    return offset_view(padded, unit_step(first, -1, 1, 0)) + offset_view(
        padded, unit_step(first, -1, -1, 0)
    )


def mixed_term(padded, first, second):
    return 0.25 * (
        offset_view(padded, unit_step(first, second, 1, 1))
        - offset_view(padded, unit_step(first, second, 1, -1))
        - offset_view(padded, unit_step(first, second, -1, 1))
        + offset_view(padded, unit_step(first, second, -1, -1))
    )


def stencil(padded, diffusion, cross_terms):
    summed = diffusion[0] * neighbours(padded, 0)
    for first in range(1, 4):
        summed = summed + diffusion[first] * neighbours(padded, first)
    for number in range(6):
        summed = summed + cross_terms[number] * mixed_term(
            padded, asset_pairs[number][0], asset_pairs[number][1]
        )
    return summed


def accumulate(totals, terms):
    if totals is None:
        return list(terms)
    return [total + term for total, term in zip(totals, terms)]


def body(value_in, payoff, diffusion, cross_terms, flags, cotangent):
    diagonal_term = 1.0 + 2.0 * jnp.sum(diffusion, axis=0)
    inner_pad = ((0, 0), (1, 1), (1, 1), (0, 0))
    saved = []
    time_step = 0
    exercised = flags[time_step] == 1
    iterate = value_in
    for sweep_index in range(SWEEPS):
        extended = extended_2(iterate, (("wide", 0), ("narrow", 3)), 1)
        padded = jnp.pad(extended, inner_pad)
        jacobi = (value_in + stencil(padded, diffusion, cross_terms)) / diagonal_term
        saved.append((padded, jacobi))
        iterate = jnp.where(exercised, payoff, jacobi)
    coupling = jnp.stack(
        [diffusion[0], diffusion[3]] + [cross_terms[number] for number in remote_pairs]
    )
    coupling_ext = extended_2(coupling, (("wide", 1), ("narrow", 4)), 1)
    coupling_ext = jnp.pad(coupling_ext, ((0, 0), (0, 0), (1, 1), (1, 1), (0, 0)))
    adjoint = cotangent
    grad_payoff = jnp.zeros_like(payoff)
    diffusion_parts = None
    cross_parts = None
    for time_step in reversed(range(STEPS)):
        exercised = flags[time_step] == 1
        back_source = jnp.zeros_like(value_in)
        for sweep_index in reversed(range(SWEEPS)):
            padded, jacobi = saved[time_step * SWEEPS + sweep_index]
            weight = jnp.where(exercised, 0.0, adjoint / diagonal_term)
            back_source = back_source + weight
            grad_payoff = grad_payoff + jnp.where(exercised, adjoint, 0.0)
            diffusion_parts = accumulate(
                diffusion_parts,
                [weight * (neighbours(padded, first) - 2.0 * jacobi) for first in range(4)],
            )
            cross_parts = accumulate(
                cross_parts,
                [
                    weight * mixed_term(padded, asset_pairs[number][0], asset_pairs[number][1])
                    for number in range(6)
                ],
            )
            weight_ext = extended_2(weight, (("wide", 0), ("narrow", 3)), 1)
            weight_ext = jnp.pad(weight_ext, inner_pad)
            remote = coupling_ext * weight_ext[None]
            local_first = jnp.pad(diffusion[1] * weight, 1)
            local_second = jnp.pad(diffusion[2] * weight, 1)
            local_cross = jnp.pad(cross_terms[3] * weight, 1)
            adjoint = neighbours(remote[0], 0) + neighbours(remote[1], 3)
            for slot in range(5):
                number = remote_pairs[slot]
                adjoint = adjoint + mixed_term(
                    remote[2 + slot], asset_pairs[number][0], asset_pairs[number][1]
                )
            adjoint = (
                adjoint
                + neighbours(local_first, 1)
                + neighbours(local_second, 2)
                + mixed_term(local_cross, 1, 2)
            )
        adjoint = adjoint + back_source
    return (adjoint, grad_payoff, jnp.stack(diffusion_parts), jnp.stack(cross_parts))


def solution(mesh):
    in_specs = (
        P("wide", None, None, "narrow"),
        P("wide", None, None, "narrow"),
        P(None, "wide", None, None, "narrow"),
        P(None, "wide", None, None, "narrow"),
        P(None, "wide", None, None, "narrow"),
        P("wide", None, None, "narrow"),
    )
    out_specs = (
        P("wide", None, None, "narrow"),
        P("wide", None, None, "narrow"),
        P(None, "wide", None, None, "narrow"),
        P(None, "wide", None, None, "narrow"),
    )
    return jax.shard_map(body, mesh=mesh, in_specs=in_specs, out_specs=out_specs, check_vma=False)
```

profile of v0, /device:TPU:56, one launch (start us, length us, event | category | flops | bytes accessed | tf_op | source)
XLA Modules:
  0.0 233.6 jit_solution(961083771325127309)
XLA Ops:
  1.7 3.4 %collective-permute-start.13 = (f32[1,16,16,128]{3,2,1,0:T(8,128)S(1)}, f32[1,16,16,128]{3,2,1,0:T(8,128)S(1)}, u32[]{:S(2)}, u32[]{:S(2)}) collective-permute-start(f32[1,16,16,128]{3,2,1,0:T(8,128)S(1)} %get-tuple-element.82), channel_id=1, source_target_pairs={{0,4},{4,8},{8,12},{12,16},{16,20},{20,24},{24,28},{28,32},{32,36}... | collective-permute-start | bytes 393224 | tf_op jit(solution)/shard_map/ppermute | solution.py:22
  5.1 8.2 %collective-permute-start.12 = (f32[1,16,16,128]{3,2,1,0:T(8,128)S(1)}, f32[1,16,16,128]{3,2,1,0:T(8,128)S(1)}, u32[]{:S(2)}, u32[]{:S(2)}) collective-permute-start(f32[1,16,16,128]{3,2,1,0:T(8,128)S(1)} %get-tuple-element.81), channel_id=1, source_target_pairs={{4,0},{8,4},{12,8},{16,12},{20,16},{24,20},{28,24},{32,28},{36,32}... | collective-permute-start | bytes 393224 | tf_op jit(solution)/shard_map/ppermute | solution.py:24
  20.7 3.6 %collective-permute-start.15 = (f32[4,16,16,1]{3,2,1,0:T(8,128)S(1)}, f32[4,16,16,1]{3,2,1,0:T(8,128)}, u32[]{:S(2)}, u32[]{:S(2)}) collective-permute-start(f32[4,16,16,1]{3,2,1,0:T(8,128)S(1)} %get-tuple-element.71), channel_id=1, source_target_pairs={{1,0},{2,1},{3,2},{5,4},{6,5},{7,6},{9,8},{10,9},{11,10},{13,12},{... | collective-permute-start | bytes 12296 | tf_op jit(solution)/shard_map/ppermute | solution.py:24
  27.7 9.3 %collective-permute-start.1 = (f32[7,1,16,16,128]{4,3,2,1,0:T(8,128)}, f32[7,1,16,16,128]{4,3,2,1,0:T(8,128)}, u32[]{:S(2)}, u32[]{:S(2)}) collective-permute-start(f32[7,1,16,16,128]{4,3,2,1,0:T(8,128)} %get-tuple-element.56), channel_id=1, source_target_pairs={{4,0},{8,4},{12,8},{16,12},{20,16},{24,20},{28,24},{32,28},{36,32}... | collective-permute-start | bytes 2752520 | tf_op jit(solution)/shard_map/ppermute | solution.py:24
  40.0 5.6 %bitcast_select_fusion = (f32[2,16,16,128]{3,2,1,0:T(8,128)S(1)}, f32[2,16,16,128]{3,2,1,0:T(8,128)}, f32[2,16,16,128]{3,2,1,0:T(8,128)}, f32[2,16,16,128]{3,2,1...) fusion(f32[2,16,16,128]{3,2,1,0:T(8,128)} %param.7, ...), kind=kLoop, calls=%fused_computation.266 | loop fusion | flops 3997696 | bytes 13180928 | tf_op jit(solution)/shard_map/jit(_where)/select_n | solution.py:95
  49.6 9.0 %collective-permute-start.5 = (f32[1,16,16,128]{3,2,1,0:T(8,128)S(1)}, f32[1,16,16,128]{3,2,1,0:T(8,128)S(1)}, u32[]{:S(2)}, u32[]{:S(2)}) collective-permute-start(f32[1,16,16,128]{3,2,1,0:T(8,128)S(1)} %get-tuple-element.78), channel_id=1, source_target_pairs={{4,0},{8,4},{12,8},{16,12},{20,16},{24,20},{28,24},{32,28},{36,32}... | collective-permute-start | bytes 393224 | tf_op jit(solution)/shard_map/ppermute | solution.py:24
  61.4 13.6 %collective-permute-done.4 = f32[1,16,16,128]{3,2,1,0:T(8,128)S(1)} collective-permute-done((f32[1,16,16,128]{3,2,1,0:T(8,128)S(1)}, f32[1,16,16,128]{3,2,1,0:T(8,128)S(1)}, u32[]{:S(2)}, u32[]{:S(2)}) %collective-permute-start.4) | collective-permute-done | bytes 131104 | tf_op jit(solution)/shard_map/ppermute | solution.py:22
  77.0 8.3 %collective-permute-done.5 = f32[1,16,16,128]{3,2,1,0:T(8,128)S(1)} collective-permute-done((f32[1,16,16,128]{3,2,1,0:T(8,128)S(1)}, f32[1,16,16,128]{3,2,1,0:T(8,128)S(1)}, u32[]{:S(2)}, u32[]{:S(2)}) %collective-permute-start.5) | collective-permute-done | bytes 131104 | tf_op jit(solution)/shard_map/ppermute | solution.py:24
  87.5 3.6 %collective-permute-start.7 = (f32[4,16,16,1]{3,2,1,0:T(8,128)S(1)}, f32[4,16,16,1]{3,2,1,0:T(8,128)S(1)}, u32[]{:S(2)}, u32[]{:S(2)}) collective-permute-start(f32[4,16,16,1]{3,2,1,0:T(8,128)S(1)} %get-tuple-element.67), channel_id=1, source_target_pairs={{1,0},{2,1},{3,2},{5,4},{6,5},{7,6},{9,8},{10,9},{11,10},{13,12},{... | collective-permute-start | bytes 12296 | tf_op jit(solution)/shard_map/ppermute | solution.py:24
  102.3 4.3 %fusion.100 = (f32[7,4,16,16,1]{4,3,2,1,0:T(8,128)}, f32[7,4,16,16,1]{4,3,2,1,0:T(8,128)}) fusion(f32[7,4,16,16,128]{4,3,2,1,0:T(8,128)S(1)} %pad_maximum_fusion.1), kind=kLoop, calls=%fused_computation.271 | loop fusion | bytes 114688 | tf_op jit(solution)/shard_map/slice | solution.py:19
  106.5 4.9 %copy.41 = f32[7,4,16,16,1]{3,2,4,1,0:T(8,128)} copy(f32[7,4,16,16,1]{4,3,2,1,0:T(8,128)} %get-tuple-element.53) | data formatting | bytes 57344
  114.1 4.9 %copy.42 = f32[7,4,16,16,1]{3,2,4,1,0:T(8,128)} copy(f32[7,4,16,16,1]{4,3,2,1,0:T(8,128)} %get-tuple-element.54) | data formatting | bytes 57344
  125.3 4.9 %copy.39 = f32[7,4,16,16,1]{4,3,2,1,0:T(8,128)} copy(f32[7,4,16,16,1]{3,2,4,1,0:T(8,128)} %collective-permute-done.2) | data formatting | bytes 57344 | tf_op jit(solution)/shard_map/ppermute | solution.py:22
  130.2 5.0 %copy.40 = f32[7,4,16,16,1]{4,3,2,1,0:T(8,128)} copy(f32[7,4,16,16,1]{3,2,4,1,0:T(8,128)} %collective-permute-done.3) | data formatting | bytes 57344 | tf_op jit(solution)/shard_map/ppermute | solution.py:24
  135.1 10.2 %pad_maximum_fusion = f32[7,4,16,16,130]{4,3,2,1,0:T(8,128)} fusion(f32[7,4,16,16,1]{4,3,2,1,0:T(8,128)} %copy.40, f32[7,1,16,16,128]{4,3,2,1,0:T(8,128)} %collective-permute-done.1, f32[2,2,16,16,128]{4,3,2,1,0:T(8,128)} %copy-done.9, f32[3,2,16,16,128]{4,3,2,1,0:T(8,128)} %copy-done.4, f32[1,2,16,16,128]{4,3,2,1,0:T(8,128)} %copy-done.16, ...), kind=kLoop, calls=%fused_computation.2 | loop fusion | flops 6522880 | bytes 7454720 | tf_op jit(solution)/shard_map/concatenate | solution.py:20
  145.3 10.2 %pad_multiply_fusion.1 = f32[7,4,18,18,130]{4,3,2,1,0:T(8,128)} fusion(f32[7,4,16,16,130]{4,3,2,1,0:T(8,128)} %pad_maximum_fusion, f32[4,18,18,130]{3,2,1,0:T(8,128)} %select_maximum_fusion.10), kind=kLoop, calls=%fused_computation.1 | loop fusion | flops 1179360 | bytes 9118720 | tf_op jit(solution)/shard_map/mul | solution.py:126
  155.5 9.4 %slice_bitcast_fusion.13 = (f32[4,18,18,130]{3,2,1,0:T(8,128)}, f32[4,18,18,130]{3,2,1,0:T(8,128)}, f32[4,18,18,130]{3,2,1,0:T(8,128)}, f32[4,18,18,130]{3,2,1,0...) fusion(f32[7,4,18,18,130]{4,3,2,1,0:T(8,128)} %pad_multiply_fusion.1), kind=kLoop, calls=%fused_computation.48 | loop fusion | bytes 9434880 | tf_op jit(solution)/shard_map/squeeze | solution.py:130
  164.9 8.4 %bitcast_dynamic-update-slice_fusion.5 = (f32[6,2,16,16,128]{4,3,2,1,0:T(8,128)}, f32[2,16,16,128]{3,2,1,0:T(8,128)S(1)}, f32[2,16,16,128]{3,2,1,0:T(8,128)S(1)}, f32[2,16,16,128]{3,2,1,0:T(8,128)S(1)}) fusion(f32[2,16,16,128]{3,2,1,0:T(8,128)S(1)} %copy-done.33, f32[2,16,16,128]{3,2,1,0:T(8,128)S(1)} %get-tuple-element.36, ...), kind=kLoop, calls=%fused_computation.208 | loop fusion | flops 3145727 | bytes 10027008
  175.5 9.4 %collective-permute-start.9 = (f32[1,16,16,128]{3,2,1,0:T(8,128)S(1)}, f32[1,16,16,128]{3,2,1,0:T(8,128)S(1)}, u32[]{:S(2)}, u32[]{:S(2)}) collective-permute-start(f32[1,16,16,128]{3,2,1,0:T(8,128)S(1)} %get-tuple-element.76), channel_id=1, source_target_pairs={{4,0},{8,4},{12,8},{16,12},{20,16},{24,20},{28,24},{32,28},{36,32}... | collective-permute-start | bytes 393224 | tf_op jit(solution)/shard_map/ppermute | solution.py:24
  198.4 3.6 %collective-permute-start.11 = (f32[4,16,16,1]{3,2,1,0:T(8,128)S(1)}, f32[4,16,16,1]{3,2,1,0:T(8,128)S(1)}, u32[]{:S(2)}, u32[]{:S(2)}) collective-permute-start(f32[4,16,16,1]{3,2,1,0:T(8,128)S(1)} %get-tuple-element.65), channel_id=1, source_target_pairs={{1,0},{2,1},{3,2},{5,4},{6,5},{7,6},{9,8},{10,9},{11,10},{13,12},{... | collective-permute-start | bytes 12296 | tf_op jit(solution)/shard_map/ppermute | solution.py:24
  203.1 3.9 %collective-permute-done.10 = f32[4,16,16,1]{3,2,1,0:T(8,128)S(1)} collective-permute-done((f32[4,16,16,1]{3,2,1,0:T(8,128)S(1)}, f32[4,16,16,1]{3,2,1,0:T(8,128)S(1)}, u32[]{:S(2)}, u32[]{:S(2)}) %collective-permute-start.10) | collective-permute-done | bytes 4128 | tf_op jit(solution)/shard_map/ppermute | solution.py:22
  209.4 9.7 %pad_multiply_fusion = f32[7,4,18,18,130]{4,3,2,1,0:T(8,128)} fusion(f32[7,4,16,16,130]{4,3,2,1,0:T(8,128)} %pad_maximum_fusion, f32[4,18,18,130]{3,2,1,0:T(8,128)S(1)} %select_maximum_fusion.6), kind=kLoop, calls=%fused_computation | loop fusion | flops 1179360 | bytes 9118720 | tf_op jit(solution)/shard_map/mul | solution.py:126
  219.1 8.1 %slice_bitcast_fusion.6 = (f32[4,18,18,130]{3,2,1,0:T(8,128)}, f32[4,18,18,130]{3,2,1,0:T(8,128)S(1)}, f32[4,18,18,130]{3,2,1,0:T(8,128)S(1)}, f32[4,18,18,130]{...) fusion(f32[7,4,18,18,130]{4,3,2,1,0:T(8,128)} %pad_multiply_fusion), kind=kLoop, calls=%fused_computation.37 | loop fusion | bytes 9434880 | tf_op jit(solution)/shard_map/squeeze | solution.py:130
  227.3 6.3 %fusion.12 = f32[2,16,16,128]{3,2,1,0:T(8,128)} fusion(f32[2,16,16,128]{3,2,1,0:T(8,128)S(1)} %copy-done.38, f32[2,16,16,128]{3,2,1,0:T(8,128)S(1)} %copy-done.39, f32[2,16,16,128]{3,2,1,0:T(8,128)S(1)} %copy-done.37, f32[4,18,18,130]{3,2,1,0:T(8,128)S(1)} %get-tuple-element.38, f32[4,18,18,130]{3,2,1,0:T(8,128)S(1)} %get-tuple-element.39, ...), kind=kLoop, calls=%fused_computation.69 | loop fusion | flops 2555904 | bytes 7864320 | tf_op jit(solution)/shard_map/add | solution.py:142
  (147 shorter events, 64.4 us)
Async XLA Ops:
  0.6 15.3 %copy-start.1 = (f32[4,2,16,16,128]{4,3,2,1,0:T(8,128)S(1)}, f32[4,2,16,16,128]{4,3,2,1,0:T(8,128)}, u32[]{:S(2)}) copy-start(f32[4,2,16,16,128]{4,3,2,1,0:T(8,128)} %param.8) | copy-start | bytes 3145732
  1.7 16.0 %collective-permute-start.13 = (f32[1,16,16,128]{3,2,1,0:T(8,128)S(1)}, f32[1,16,16,128]{3,2,1,0:T(8,128)S(1)}, u32[]{:S(2)}, u32[]{:S(2)}) collective-permute-start(f32[1,16,16,128]{3,2,1,0:T(8,128)S(1)} %get-tuple-element.82), channel_id=1, source_target_pairs={{0,4},{4,8},{8,12},{12,16},{16,20},{20,24},{24,28},{28,32},{32,36}... | collective-permute-start | bytes 393224 | tf_op jit(solution)/shard_map/ppermute | solution.py:22
  5.1 12.6 %collective-permute-start.12 = (f32[1,16,16,128]{3,2,1,0:T(8,128)S(1)}, f32[1,16,16,128]{3,2,1,0:T(8,128)S(1)}, u32[]{:S(2)}, u32[]{:S(2)}) collective-permute-start(f32[1,16,16,128]{3,2,1,0:T(8,128)S(1)} %get-tuple-element.81), channel_id=1, source_target_pairs={{4,0},{8,4},{12,8},{16,12},{20,16},{24,20},{28,24},{32,28},{36,32}... | collective-permute-start | bytes 393224 | tf_op jit(solution)/shard_map/ppermute | solution.py:24
  17.7 22.3 %copy-start.24 = (f32[1,16,16,128]{3,2,1,0:T(8,128)}, f32[1,16,16,128]{3,2,1,0:T(8,128)S(1)}, u32[]{:S(2)}) copy-start(f32[1,16,16,128]{3,2,1,0:T(8,128)S(1)} %collective-permute-done.13) | copy-start | bytes 393220
  18.8 18.3 %collective-permute-start.14 = (f32[4,16,16,1]{3,2,1,0:T(8,128)}, f32[4,16,16,1]{3,2,1,0:T(8,128)S(1)}, u32[]{:S(2)}, u32[]{:S(2)}) collective-permute-start(f32[4,16,16,1]{3,2,1,0:T(8,128)} %get-tuple-element.70), channel_id=1, source_target_pairs={{0,1},{1,2},{2,3},{4,5},{5,6},{6,7},{8,9},{9,10},{10,11},{12,13},{... | collective-permute-start | bytes 12296 | tf_op jit(solution)/shard_map/ppermute | solution.py:22
  20.7 17.2 %collective-permute-start.15 = (f32[4,16,16,1]{3,2,1,0:T(8,128)S(1)}, f32[4,16,16,1]{3,2,1,0:T(8,128)}, u32[]{:S(2)}, u32[]{:S(2)}) collective-permute-start(f32[4,16,16,1]{3,2,1,0:T(8,128)S(1)} %get-tuple-element.71), channel_id=1, source_target_pairs={{1,0},{2,1},{3,2},{5,4},{6,5},{7,6},{9,8},{10,9},{11,10},{13,12},{... | collective-permute-start | bytes 12296 | tf_op jit(solution)/shard_map/ppermute | solution.py:24
  25.8 74.7 %collective-permute-start = (f32[7,1,16,16,128]{4,3,2,1,0:T(8,128)}, f32[7,1,16,16,128]{4,3,2,1,0:T(8,128)}, u32[]{:S(2)}, u32[]{:S(2)}) collective-permute-start(f32[7,1,16,16,128]{4,3,2,1,0:T(8,128)} %get-tuple-element.55), channel_id=1, source_target_pairs={{0,4},{4,8},{8,12},{12,16},{16,20},{20,24},{24,28},{28,32},{32,36}... | collective-permute-start | bytes 2752520 | tf_op jit(solution)/shard_map/ppermute | solution.py:22
  27.7 72.8 %collective-permute-start.1 = (f32[7,1,16,16,128]{4,3,2,1,0:T(8,128)}, f32[7,1,16,16,128]{4,3,2,1,0:T(8,128)}, u32[]{:S(2)}, u32[]{:S(2)}) collective-permute-start(f32[7,1,16,16,128]{4,3,2,1,0:T(8,128)} %get-tuple-element.56), channel_id=1, source_target_pairs={{4,0},{8,4},{12,8},{16,12},{20,16},{24,20},{28,24},{32,28},{36,32}... | collective-permute-start | bytes 2752520 | tf_op jit(solution)/shard_map/ppermute | solution.py:24
  45.7 76.4 %copy-start.7 = (f32[2,16,16,128]{3,2,1,0:T(8,128)}, f32[2,16,16,128]{3,2,1,0:T(8,128)S(1)}, u32[]{:S(2)}) copy-start(f32[2,16,16,128]{3,2,1,0:T(8,128)S(1)} %get-tuple-element.25) | copy-start | bytes 786436
  47.6 27.4 %collective-permute-start.4 = (f32[1,16,16,128]{3,2,1,0:T(8,128)S(1)}, f32[1,16,16,128]{3,2,1,0:T(8,128)S(1)}, u32[]{:S(2)}, u32[]{:S(2)}) collective-permute-start(f32[1,16,16,128]{3,2,1,0:T(8,128)S(1)} %get-tuple-element.77), channel_id=1, source_target_pairs={{0,4},{4,8},{8,12},{12,16},{16,20},{20,24},{24,28},{28,32},{32,36}... | collective-permute-start | bytes 393224 | tf_op jit(solution)/shard_map/ppermute | solution.py:22
  49.6 35.7 %collective-permute-start.5 = (f32[1,16,16,128]{3,2,1,0:T(8,128)S(1)}, f32[1,16,16,128]{3,2,1,0:T(8,128)S(1)}, u32[]{:S(2)}, u32[]{:S(2)}) collective-permute-start(f32[1,16,16,128]{3,2,1,0:T(8,128)S(1)} %get-tuple-element.78), channel_id=1, source_target_pairs={{4,0},{8,4},{12,8},{16,12},{20,16},{24,20},{28,24},{32,28},{36,32}... | collective-permute-start | bytes 393224 | tf_op jit(solution)/shard_map/ppermute | solution.py:24
  58.6 28.8 %collective-permute-start.16 = (f32[1,16,16,128]{3,2,1,0:T(8,128)S(1)}, f32[1,16,16,128]{3,2,1,0:T(8,128)S(1)}, u32[]{:S(2)}, u32[]{:S(2)}) collective-permute-start(f32[1,16,16,128]{3,2,1,0:T(8,128)S(1)} %get-tuple-element.80), channel_id=1, source_target_pairs={{4,0},{8,4},{12,8},{16,12},{20,16},{24,20},{28,24},{32,28},{36,32}... | collective-permute-start | bytes 393224 | tf_op jit(solution)/shard_map/ppermute | solution.py:24
  75.1 16.1 %collective-permute-start.17 = (f32[1,16,16,128]{3,2,1,0:T(8,128)S(1)}, f32[1,16,16,128]{3,2,1,0:T(8,128)S(1)}, u32[]{:S(2)}, u32[]{:S(2)}) collective-permute-start(f32[1,16,16,128]{3,2,1,0:T(8,128)S(1)} %get-tuple-element.79), channel_id=1, source_target_pairs={{0,4},{4,8},{8,12},{12,16},{16,20},{20,24},{24,28},{28,32},{32,36}... | collective-permute-start | bytes 393224 | tf_op jit(solution)/shard_map/ppermute | solution.py:22
  85.6 10.5 %collective-permute-start.6 = (f32[4,16,16,1]{3,2,1,0:T(8,128)S(1)}, f32[4,16,16,1]{3,2,1,0:T(8,128)S(1)}, u32[]{:S(2)}, u32[]{:S(2)}) collective-permute-start(f32[4,16,16,1]{3,2,1,0:T(8,128)S(1)} %get-tuple-element.66), channel_id=1, source_target_pairs={{0,1},{1,2},{2,3},{4,5},{5,6},{6,7},{8,9},{9,10},{10,11},{12,13},{... | collective-permute-start | bytes 12296 | tf_op jit(solution)/shard_map/ppermute | solution.py:22
  87.5 11.0 %collective-permute-start.7 = (f32[4,16,16,1]{3,2,1,0:T(8,128)S(1)}, f32[4,16,16,1]{3,2,1,0:T(8,128)S(1)}, u32[]{:S(2)}, u32[]{:S(2)}) collective-permute-start(f32[4,16,16,1]{3,2,1,0:T(8,128)S(1)} %get-tuple-element.67), channel_id=1, source_target_pairs={{1,0},{2,1},{3,2},{5,4},{6,5},{7,6},{9,8},{10,9},{11,10},{13,12},{... | collective-permute-start | bytes 12296 | tf_op jit(solution)/shard_map/ppermute | solution.py:24
  92.4 29.6 %collective-permute-start.18 = (f32[4,16,16,1]{3,2,1,0:T(8,128)}, f32[4,16,16,1]{3,2,1,0:T(8,128)}, u32[]{:S(2)}, u32[]{:S(2)}) collective-permute-start(f32[4,16,16,1]{3,2,1,0:T(8,128)} %get-tuple-element.68), channel_id=1, source_target_pairs={{0,1},{1,2},{2,3},{4,5},{5,6},{6,7},{8,9},{9,10},{10,11},{12,13},{... | collective-permute-start | bytes 12296 | tf_op jit(solution)/shard_map/ppermute | solution.py:22
  96.1 26.0 %collective-permute-start.19 = (f32[4,16,16,1]{3,2,1,0:T(8,128)}, f32[4,16,16,1]{3,2,1,0:T(8,128)}, u32[]{:S(2)}, u32[]{:S(2)}) collective-permute-start(f32[4,16,16,1]{3,2,1,0:T(8,128)} %get-tuple-element.69), channel_id=1, source_target_pairs={{1,0},{2,1},{3,2},{5,4},{6,5},{7,6},{9,8},{10,9},{11,10},{13,12},{... | collective-permute-start | bytes 12296 | tf_op jit(solution)/shard_map/ppermute | solution.py:24
  111.4 13.9 %collective-permute-start.2 = (f32[7,4,16,16,1]{3,2,4,1,0:T(8,128)}, f32[7,4,16,16,1]{3,2,4,1,0:T(8,128)}, u32[]{:S(2)}, u32[]{:S(2)}) collective-permute-start(f32[7,4,16,16,1]{3,2,4,1,0:T(8,128)} %copy.41), channel_id=1, source_target_pairs={{0,1},{1,2},{2,3},{4,5},{5,6},{6,7},{8,9},{9,10},{10,11},{12,13},{... | collective-permute-start | bytes 86024 | tf_op jit(solution)/shard_map/ppermute | solution.py:22
  119.0 11.2 %collective-permute-start.3 = (f32[7,4,16,16,1]{3,2,4,1,0:T(8,128)}, f32[7,4,16,16,1]{3,2,4,1,0:T(8,128)}, u32[]{:S(2)}, u32[]{:S(2)}) collective-permute-start(f32[7,4,16,16,1]{3,2,4,1,0:T(8,128)} %copy.42), channel_id=1, source_target_pairs={{1,0},{2,1},{3,2},{5,4},{6,5},{7,6},{9,8},{10,9},{11,10},{13,12},{... | collective-permute-start | bytes 86024 | tf_op jit(solution)/shard_map/ppermute | solution.py:24
  164.9 20.0 %copy-start.32 = (f32[2,16,16,128]{3,2,1,0:T(8,128)S(1)}, f32[2,16,16,128]{3,2,1,0:T(8,128)}, u32[]{:S(2)}) copy-start(f32[2,16,16,128]{3,2,1,0:T(8,128)} %get-tuple-element.29) | copy-start | bytes 786436
  173.4 22.8 %collective-permute-start.8 = (f32[1,16,16,128]{3,2,1,0:T(8,128)S(1)}, f32[1,16,16,128]{3,2,1,0:T(8,128)S(1)}, u32[]{:S(2)}, u32[]{:S(2)}) collective-permute-start(f32[1,16,16,128]{3,2,1,0:T(8,128)S(1)} %get-tuple-element.75), channel_id=1, source_target_pairs={{0,4},{4,8},{8,12},{12,16},{16,20},{20,24},{24,28},{28,32},{32,36}... | collective-permute-start | bytes 393224 | tf_op jit(solution)/shard_map/ppermute | solution.py:22
  175.5 20.8 %collective-permute-start.9 = (f32[1,16,16,128]{3,2,1,0:T(8,128)S(1)}, f32[1,16,16,128]{3,2,1,0:T(8,128)S(1)}, u32[]{:S(2)}, u32[]{:S(2)}) collective-permute-start(f32[1,16,16,128]{3,2,1,0:T(8,128)S(1)} %get-tuple-element.76), channel_id=1, source_target_pairs={{4,0},{8,4},{12,8},{16,12},{20,16},{24,20},{28,24},{32,28},{36,32}... | collective-permute-start | bytes 393224 | tf_op jit(solution)/shard_map/ppermute | solution.py:24
  196.5 10.5 %collective-permute-start.10 = (f32[4,16,16,1]{3,2,1,0:T(8,128)S(1)}, f32[4,16,16,1]{3,2,1,0:T(8,128)S(1)}, u32[]{:S(2)}, u32[]{:S(2)}) collective-permute-start(f32[4,16,16,1]{3,2,1,0:T(8,128)S(1)} %get-tuple-element.64), channel_id=1, source_target_pairs={{0,1},{1,2},{2,3},{4,5},{5,6},{6,7},{8,9},{9,10},{10,11},{12,13},{... | collective-permute-start | bytes 12296 | tf_op jit(solution)/shard_map/ppermute | solution.py:22
  198.4 10.3 %collective-permute-start.11 = (f32[4,16,16,1]{3,2,1,0:T(8,128)S(1)}, f32[4,16,16,1]{3,2,1,0:T(8,128)S(1)}, u32[]{:S(2)}, u32[]{:S(2)}) collective-permute-start(f32[4,16,16,1]{3,2,1,0:T(8,128)S(1)} %get-tuple-element.65), channel_id=1, source_target_pairs={{1,0},{2,1},{3,2},{5,4},{6,5},{7,6},{9,8},{10,9},{11,10},{13,12},{... | collective-permute-start | bytes 12296 | tf_op jit(solution)/shard_map/ppermute | solution.py:24
  (37 other events, 197.8 us)
where the time goes:
time: 238 us; the launch traced here: 234 us
  starting transfers between devices  76 us (32%)
  other arithmetic  74.8 us (31%)
  local copies, waits for them, and re-layouts  51.5 us (22%)
  waiting for transfers between devices  30 us (13%)
    ppermute x10, starting transfers between devices, extended_2(): lax.ppermute(head, axis, [((i + 1) % count, i) for i in range(ends)])  54.3 us
    ppermute x10, starting transfers between devices, extended_2(): lax.ppermute(tail, axis, [(i, (i + 1) % count) for i in range(ends)])  21.7 us
    concatenate x9, other arithmetic, extended_2(): jnp.concatenate([lax.ppermute(tail, axis, [(i, (i + 1) % count) for i in...  19.9 us
    mul x2, other arithmetic, body(): remote = coupling_ext * weight_ext[None]  19.9 us
    ppermute x10, waiting for transfers between devices, extended_2(): lax.ppermute(tail, axis, [(i, (i + 1) % count) for i in range(ends)])  19.9 us
    squeeze x2, local copies, waits for them, and re-layouts, body(): adjoint = neighbours(remote[0], 0) + neighbours(remote[1], 3)  17.5 us
    unnamed x5, other arithmetic  13.9 us
    unnamed x86, local copies, waits for them, and re-layouts  12.1 us
  transfers between devices with their start and end apart: 20, of which 6 were waited for; matrix products, arithmetic and copies ran while one was open for 23% of the time, Pallas kernels for 0%

commit v1 on v0

v1 whole, which is shorter than its diff:
```python
import functools
import jax
import jax.numpy as jnp
from jax import lax
from jax.experimental import pallas as pl
from jax.experimental.pallas import tpu as pltpu
from jax.sharding import PartitionSpec as P

F32 = jnp.float32
TILE = (16, 128)
BLOCK = (2, 16, 16, 128)


def lanes():
    return lax.broadcasted_iota(jnp.int32, TILE, 1)


def rows():
    return lax.broadcasted_iota(jnp.int32, TILE, 0)


def lane_roll(x, shift):
    shift = shift % 128
    return x if shift == 0 else pltpu.roll(x, shift, 1)


def up2(x, row):
    return jnp.where(row == 15, 0.0, pltpu.roll(x, 15, 0))


def down2(x, row):
    return jnp.where(row == 0, 0.0, pltpu.roll(x, 1, 0))


def wide_odd():
    return lax.rem(lax.axis_index("wide"), 2)


def narrow_odd():
    return lax.rem(lax.axis_index("narrow"), 2)


def adjoint(w_of, u_of, dif, crs, scratch, msg_a, msg_b, n1, n2, adj_of):
    q1s, p01s, p12s, p13s, x2s, y2s, x3s, y3s, q0s, p02s, p03s = scratch
    row, lane = rows(), lanes()
    zero = jnp.zeros(TILE, F32)
    for ref in (q1s, p01s, p12s, p13s):
        for r in range(2):
            ref[r, 0] = zero
            ref[r, 17] = zero
    for i in range(16):
        w = [w_of(r, i) for r in range(2)]
        h = [0.25 * w[r] for r in range(2)]
        p02 = [crs[1, r, i] * h[r] for r in range(2)]
        p03 = [crs[2, r, i] * h[r] for r in range(2)]
        for r in range(2):
            q0s[r, i] = dif[0, r, i] * w[r]
            q1s[r, i + 1] = dif[1, r, i] * w[r]
            p01s[r, i + 1] = crs[0, r, i] * h[r]
            p12s[r, i + 1] = crs[3, r, i] * h[r]
            p13s[r, i + 1] = crs[4, r, i] * h[r]
            p02s[r, i] = p02[r]
            p03s[r, i] = p03[r]
            q2 = dif[2, r, i] * w[r]
            e02 = p02[1] if r == 0 else -p02[0]
            x2s[r, i] = q2 + e02
            y2s[r, i] = q2 - e02
            q3 = dif[3, r, i] * w[r]
            p23 = crs[5, r, i] * h[r]
            e3 = (p03[1] if r == 0 else -p03[0]) + (up2(p23, row) - down2(p23, row))
            x3s[r, i] = q3 + e3
            y3s[r, i] = q3 - e3
    odd = wide_odd()
    row_a = 1 - odd
    row_b = odd
    sign_a = (2 * odd - 1).astype(F32)
    left = jnp.zeros(TILE, F32)
    right = jnp.zeros(TILE, F32)

    def put(packed, value, source, column):
        return jnp.where(lane == column, lane_roll(value, column - source), packed)

    for i in range(16):
        for r in range(2):
            u = u_of(r, i)
            left = put(left, u, 0, r * 16 + i)
            right = put(right, u, 127, r * 16 + i)
            f12 = p12s[r, i + 2] - p12s[r, i]
            f13 = p13s[r, i + 2] - p13s[r, i]
            x3 = x3s[r, i] + f13
            y3 = y3s[r, i] - f13
            x2 = x2s[r, i] + f12
            y2 = y2s[r, i] - f12
            e01 = p01s[1 - r, i + 2] - p01s[1 - r, i]
            total = q0s[1 - r, i] + q1s[r, i + 2] + q1s[r, i]
            total = total + e01 if r == 0 else total - e01
            total = total + up2(x2, row) + down2(y2, row)
            total = total + jnp.where(lane == 127, 0.0, lane_roll(x3, 127)) + jnp.where(lane == 0, 0.0, lane_roll(y3, 1))
            adj_of(r, i, total)
            left = put(left, x3, 0, 48 + r * 16 + i)
            right = put(right, y3, 127, 48 + r * 16 + i)
        p0, p1 = p03s[0, i], p03s[1, i]
        left = put(left, p0, 0, 32 + i)
        right = put(right, -p0, 127, 32 + i)
        left = put(left, -p1, 0, 80 + i)
        right = put(right, p1, 127, 80 + i)
        for msg, at, sign in ((msg_a, row_a, sign_a), (msg_b, row_b, -sign_a)):
            p02, p03 = p02s[at, i], p03s[at, i]
            d = p01s[at, i + 2] - p01s[at, i]
            d = d + up2(p02, row) - down2(p02, row)
            d = d + jnp.where(lane == 127, 0.0, lane_roll(p03, 127)) - jnp.where(lane == 0, 0.0, lane_roll(p03, 1))
            msg[1, i] = q0s[at, i] + sign * d
            msg[0, i] = u_of(at, i)
    even = narrow_odd() == 0
    n1[...] = jnp.where(even, right, left)
    n2[...] = jnp.where(even, left, right)


def stencil(fill, recv_a, recv_b, r1, r2, cor_a, cor_b, scratch, use):
    us, d2s, d3s, n2s, n3s = scratch
    row, lane = rows(), lanes()
    zero = jnp.zeros(TILE, F32)
    for r in range(4):
        for ref in (us, d2s, d3s):
            ref[r, 0] = zero
            ref[r, 17] = zero
    fill(us)
    odd = wide_odd()
    at_a, at_b = 3 * (1 - odd), 3 * odd
    us[at_a, 1:17] = recv_a[0]
    us[at_b, 1:17] = recv_b[0]
    even_n = narrow_odd() == 0
    even_w = odd == 0
    first, second = r1[...], r2[...]
    from_right = jnp.where(even_n, first, second)
    from_left = jnp.where(even_n, second, first)
    a0, a1, b0, b1 = cor_a[0], cor_a[1], cor_b[0], cor_b[1]
    a_right, a_left = jnp.where(even_n, a0, a1), jnp.where(even_n, a1, a0)
    b_right, b_left = jnp.where(even_n, b0, b1), jnp.where(even_n, b1, b0)
    low_right, low_left = jnp.where(even_w, b_right, a_right), jnp.where(even_w, b_left, a_left)
    high_right, high_left = jnp.where(even_w, a_right, b_right), jnp.where(even_w, a_left, b_left)
    packs = (
        (low_right, low_left, 16),
        (from_right, from_left, 0),
        (from_right, from_left, 16),
        (high_right, high_left, 0),
    )
    for i in range(16):
        for r in range(4):
            x = us[r, i + 1]
            pack_right, pack_left, base = packs[r]
            plus = jnp.where(lane == 127, lane_roll(pack_right, 127 - base - i), lane_roll(x, 127))
            minus = jnp.where(lane == 0, lane_roll(pack_left, -base - i), lane_roll(x, 1))
            d3s[r, i + 1] = plus - minus
            above, below = up2(x, row), down2(x, row)
            d2s[r, i + 1] = above - below
            if r in (1, 2):
                n3s[r - 1, i] = plus + minus
                n2s[r - 1, i] = above + below
    for i in range(16):
        d1 = [us[r, i + 2] - us[r, i] for r in range(4)]
        for r in range(2):
            c = r + 1
            d3 = d3s[c, i + 1]
            sums = (us[c + 1, i + 1] + us[c - 1, i + 1], us[c, i + 2] + us[c, i], n2s[r, i], n3s[r, i])
            mixed = (
                0.25 * (d1[c + 1] - d1[c - 1]),
                0.25 * (d2s[c + 1, i + 1] - d2s[c - 1, i + 1]),
                0.25 * (d3s[c + 1, i + 1] - d3s[c - 1, i + 1]),
                0.25 * (d2s[c, i + 2] - d2s[c, i]),
                0.25 * (d3s[c, i + 2] - d3s[c, i]),
                0.25 * (up2(d3, row) - down2(d3, row)),
            )
            use(r, i, sums, mixed)


def overhang(recv_a, recv_b, r1, r2, cor_a, cor_b, local, put):
    lane = lanes()
    even_w = wide_odd() == 0
    even_n = narrow_odd() == 0
    first, second = r1[...], r2[...]
    from_right = jnp.where(even_n, first, second)
    from_left = jnp.where(even_n, second, first)
    a0, a1, b0, b1 = cor_a[0], cor_a[1], cor_b[0], cor_b[1]
    a_right, a_left = jnp.where(even_n, a0, a1), jnp.where(even_n, a1, a0)
    b_right, b_left = jnp.where(even_n, b0, b1), jnp.where(even_n, b1, b0)
    low_right, low_left = jnp.where(even_w, b_right, a_right), jnp.where(even_w, b_left, a_left)
    high_right, high_left = jnp.where(even_w, a_right, b_right), jnp.where(even_w, a_left, b_left)

    def gathered(own, low, high):
        return lane_roll(own, -48) + jnp.where(lane < 16, lane_roll(low, -80), lane_roll(high, -16))

    cols_right = gathered(from_right, low_right, high_right)
    cols_left = gathered(from_left, low_left, high_left)
    odd = wide_odd()
    for i in range(16):
        for r in range(2):
            wide = jnp.where(even_w, recv_b[1, i], recv_a[1, i]) if r == 0 else jnp.where(even_w, recv_a[1, i], recv_b[1, i])
            at = r * 16 + i
            column = jnp.where(lane == 127, lane_roll(cols_right, 127 - at), jnp.where(lane == 0, lane_roll(cols_left, -at), 0.0))
            put(r, i, local(r, i) + wide + column)


ADJOINT_SCRATCH = [pltpu.VMEM((2, 18, *TILE), F32)] * 4 + [pltpu.VMEM(BLOCK, F32)] * 7
STENCIL_SCRATCH = [pltpu.VMEM((4, 18, *TILE), F32)] * 3 + [pltpu.VMEM(BLOCK, F32)] * 2


def kernel_a(cot, flg, dif, crs, val, msg_a, msg_b, n1, n2, inv, w2, adj, *scratch):
    def weight(r, i):
        recip = 1.0 / (1.0 + 2.0 * (dif[0, r, i] + dif[1, r, i] + dif[2, r, i] + dif[3, r, i]))
        inv[r, i] = recip
        w = jnp.where(flg[r, i] == 1, 0.0, cot[r, i] * recip)
        w2[r, i] = w
        return w

    def keep(r, i, total):
        adj[r, i] = total

    adjoint(weight, lambda r, i: val[r, i], dif, crs, scratch, msg_a, msg_b, n1, n2, keep)


def kernel_b(val, pay, flg, dif, crs, inv, adj_in, ra, rb, r1, r2, ca, cb, msg_a, msg_b, n1, n2, u1, w1, adj1, adj0, *scratch):
    def fill(us):
        us[1:3, 1:17] = val[...]

    def use(r, i, sums, mixed):
        total = val[r, i]
        for k in range(4):
            total = total + dif[k, r, i] * sums[k]
        for k in range(6):
            total = total + crs[k, r, i] * mixed[k]
        u1[r, i] = jnp.where(flg[r, i] == 1, pay[r, i], total * inv[r, i])

    stencil(fill, ra, rb, r1, r2, ca, cb, scratch[:5], use)

    def put(r, i, total):
        adj1[r, i] = total
        w1[r, i] = jnp.where(flg[r, i] == 1, 0.0, total * inv[r, i])

    overhang(ra, rb, r1, r2, ca, cb, lambda r, i: adj_in[r, i], put)

    def keep(r, i, total):
        adj0[r, i] = total

    adjoint(lambda r, i: w1[r, i], lambda r, i: u1[r, i], dif, crs, scratch[5:], msg_a, msg_b, n1, n2, keep)


def kernel_m(val, flg, dif, crs, inv, w1, w2, cot, adj1, adj0, ra, rb, r1, r2, ca, cb, gpay, part, gd, gc, *scratch):
    def fill(us):
        us[1:3, 1:17] = val[...]

    def use(r, i, sums, mixed):
        total = val[r, i]
        for k in range(4):
            total = total + dif[k, r, i] * sums[k]
        for k in range(6):
            total = total + crs[k, r, i] * mixed[k]
        twice = 2.0 * (total * inv[r, i])
        w = w1[r, i]
        for k in range(4):
            gd[k, r, i] = w * (sums[k] - twice)
        for k in range(6):
            gc[k, r, i] = w * mixed[k]
        gpay[r, i] = jnp.where(flg[r, i] == 1, cot[r, i] + adj1[r, i], 0.0)
        part[r, i] = adj0[r, i] + w + w2[r, i]

    stencil(fill, ra, rb, r1, r2, ca, cb, scratch, use)


def kernel_c(val, u1, dif, crs, inv, w2, part, pd, pc, ra, rb, r1, r2, ca, cb, gval, gd, gc, *scratch):
    def fill(us):
        us[1:3, 1:17] = u1[...]

    def use(r, i, sums, mixed):
        total = val[r, i]
        for k in range(4):
            total = total + dif[k, r, i] * sums[k]
        for k in range(6):
            total = total + crs[k, r, i] * mixed[k]
        twice = 2.0 * (total * inv[r, i])
        w = w2[r, i]
        for k in range(4):
            gd[k, r, i] = pd[k, r, i] + w * (sums[k] - twice)
        for k in range(6):
            gc[k, r, i] = pc[k, r, i] + w * mixed[k]

    stencil(fill, ra, rb, r1, r2, ca, cb, scratch, use)

    def put(r, i, total):
        gval[r, i] = total

    overhang(ra, rb, r1, r2, ca, cb, lambda r, i: part[r, i], put)


def call(kernel, outs, scratch, flops, *args):
    return pl.pallas_call(
        kernel,
        out_shape=[jax.ShapeDtypeStruct(shape, F32) for shape in outs],
        in_specs=[pl.BlockSpec(memory_space=pltpu.VMEM)] * len(args),
        out_specs=[pl.BlockSpec(memory_space=pltpu.VMEM)] * len(outs),
        scratch_shapes=scratch,
        cost_estimate=pl.CostEstimate(flops=flops, bytes_accessed=4 << 20, transcendentals=0),
        compiler_params=pltpu.CompilerParams(vmem_limit_bytes=40 << 20),
    )(*args)


def swap(x, axis, odd, count):
    pairs = []
    for i in range(odd, count - 1, 2):
        pairs += [(i, i + 1), (i + 1, i)]
    return lax.ppermute(x, axis, pairs)


def exchange(msg_a, msg_b, n1, n2):
    wide, narrow = lax.axis_size("wide"), lax.axis_size("narrow")
    rb = swap(msg_b, "wide", 1, wide)
    ra = swap(msg_a, "wide", 0, wide)
    r1 = swap(n1, "narrow", 0, narrow)
    r2 = swap(n2, "narrow", 1, narrow)
    corners = jnp.stack([r1, r2])
    cb = swap(corners, "wide", 1, wide)
    ca = swap(corners, "wide", 0, wide)
    return ra, rb, r1, r2, ca, cb


def body(value_in, payoff, diffusion, cross_terms, flags, cotangent):
    flg = flags[0]
    message = (2, 16, *TILE)
    sends = [message, message, TILE, TILE]
    msg_a, msg_b, n1, n2, inv, w2, adj = call(
        kernel_a, sends + [BLOCK] * 3, ADJOINT_SCRATCH, 40 << 16, cotangent, flg, diffusion, cross_terms, value_in
    )
    first = exchange(msg_a, msg_b, n1, n2)
    msg_a, msg_b, n1, n2, u1, w1, adj1, adj0 = call(
        kernel_b, sends + [BLOCK] * 4, STENCIL_SCRATCH + ADJOINT_SCRATCH, 80 << 16, value_in, payoff, flg, diffusion, cross_terms, inv, adj, *first
    )
    second = exchange(msg_a, msg_b, n1, n2)
    gpay, part, pd, pc = call(
        kernel_m, [BLOCK, BLOCK, (4, *BLOCK), (6, *BLOCK)], STENCIL_SCRATCH, 60 << 16,
        value_in, flg, diffusion, cross_terms, inv, w1, w2, cotangent, adj1, adj0, *first,
    )
    gval, gd, gc = call(
        kernel_c, [BLOCK, (4, *BLOCK), (6, *BLOCK)], STENCIL_SCRATCH, 60 << 16,
        value_in, u1, diffusion, cross_terms, inv, w2, part, pd, pc, *second,
    )
    return gval, gpay, gd, gc


def solution(mesh):
    field = P("wide", None, None, "narrow")
    stack = P(None, "wide", None, None, "narrow")
    return jax.shard_map(
        body, mesh=mesh, in_specs=(field, field, stack, stack, stack, field), out_specs=(field, field, stack, stack), check_vma=False
    )
```

time: 238 us -> 65.1 us (0.27); the launches traced: 234 us -> 64.7 us
  other arithmetic: 74.8 us -> 0.01 us
  local copies, waits for them, and re-layouts: 51.5 us -> 5.48 us
  starting transfers between devices: 76 us -> 31.4 us
  waiting for transfers between devices: 30 us -> 20.4 us
  Pallas kernels: 0 us -> 6.64 us
    ppermute x20 -> x12, starting transfers between devices: 76 us -> 31.4 us  [swap(): return lax.ppermute(x, axis, pairs)]
    mul x4 -> x0, other arithmetic: 22.6 us -> none  [the longest x2 19.9 us: body(): remote = coupling_ext * weight_ext[None]]
    concatenate x9 -> x0, other arithmetic: 19.9 us -> none  [extended_2(): jnp.concatenate([lax.ppermute(tail, axis, [(i, (i + 1) % count) for i in...]
    squeeze x2 -> x0, local copies, waits for them, and re-layouts: 17.5 us -> none  [body(): adjoint = neighbours(remote[0], 0) + neighbours(remote[1], 3)]
    unnamed x5 -> x0, other arithmetic: 13.9 us -> none
    slice x13 -> x0, local copies, waits for them, and re-layouts: 12.1 us -> none  [the longest x9 8.38 us: extended_2(): lax.slice_in_dim(cells, cells.shape[dim] - width, cells.shape[dim], axis=...]
    ppermute x2 -> x0, local copies, waits for them, and re-layouts: 9.82 us -> none  [the longest x1 4.96 us: extended_2(): lax.ppermute(head, axis, [((i + 1) % count, i) for i in range(ends)])]
    ppermute x20 -> x12, waiting for transfers between devices: 30 us -> 20.4 us  [swap(): return lax.ppermute(x, axis, pairs)]
  transfers between devices with their start and end apart: 20 -> 12, of which waited for: 6 -> 4; matrix products, arithmetic and copies ran while one was open for 23% -> 0% of each run, Pallas kernels for 0% -> 2%
where the time goes in v1:
time: 65.1 us; the launch traced here: 64.7 us
  starting transfers between devices  31.4 us (48%)
  waiting for transfers between devices  20.4 us (31%)
  Pallas kernels  6.64 us (10%)
  local copies, waits for them, and re-layouts  5.48 us (8%)
  between operations  0.79 us (1%)
    ppermute x12, starting transfers between devices, swap(): return lax.ppermute(x, axis, pairs)  31.4 us
    ppermute x12, waiting for transfers between devices, swap(): return lax.ppermute(x, axis, pairs)  20.4 us
    pallas_call x4, Pallas kernels, call(): pl.pallas_call(kernel, out_shape=[jax.ShapeDtypeStruct(shape, F32) for sh...  6.64 us
    unnamed x16, local copies, waits for them, and re-layouts  5.48 us
  transfers between devices with their start and end apart: 12, of which 4 were waited for; matrix products, arithmetic and copies ran while one was open for 0% of the time, Pallas kernels for 2%

profile of v1, /device:TPU:56, one launch (start us, length us, event | category | flops | bytes accessed | tf_op | source)
XLA Modules:
  0.0 64.7 jit_solution(10369316852555834307)
XLA Ops:
  0.6 1.4 %copy-done = f32[6,2,16,16,128]{4,3,2,1,0:T(8,128)S(1)} copy-done((f32[6,2,16,16,128]{4,3,2,1,0:T(8,128)S(1)}, f32[6,2,16,16,128]{4,3,2,1,0:T(8,128)}, u32[]{:S(2)}) %copy-start) | copy-done | bytes 1572888
  2.0 1.2 %copy-done.2 = f32[4,2,16,16,128]{4,3,2,1,0:T(8,128)S(1)} copy-done((f32[4,2,16,16,128]{4,3,2,1,0:T(8,128)S(1)}, f32[4,2,16,16,128]{4,3,2,1,0:T(8,128)}, u32[]{:S(2)}) %copy-start.2) | copy-done | bytes 1048600
  3.3 0.9 %copy-done.3 = f32[2,16,16,128]{3,2,1,0:T(8,128)S(1)} copy-done((f32[2,16,16,128]{3,2,1,0:T(8,128)S(1)}, f32[2,16,16,128]{3,2,1,0:T(8,128)}, u32[]{:S(2)}) %copy-start.3) | copy-done | bytes 262168
  4.2 0.9 %copy-done.5 = s32[1,2,16,16,128]{4,3,2,1,0:T(8,128)S(1)} copy-done((s32[1,2,16,16,128]{4,3,2,1,0:T(8,128)S(1)}, s32[1,2,16,16,128]{4,3,2,1,0:T(8,128)}, u32[]{:S(2)}) %copy-start.5) | copy-done | bytes 262168
  5.2 0.9 %copy-done.6 = f32[2,16,16,128]{3,2,1,0:T(8,128)S(1)} copy-done((f32[2,16,16,128]{3,2,1,0:T(8,128)S(1)}, f32[2,16,16,128]{3,2,1,0:T(8,128)}, u32[]{:S(2)}) %copy-start.6) | copy-done | bytes 262168
  6.1 0.8 %shard_map.93 = (f32[2,16,16,128]{3,2,1,0:T(8,128)S(1)}, f32[2,16,16,128]{3,2,1,0:T(8,128)S(1)}, f32[16,128]{1,0:T(8,128)S(1)}, f32[16,128]{1,0:T(8,128)S(1)}, f...) custom-call(f32[2,16,16,128]{3,2,1,0:T(8,128)S(1)} %copy-done.6, ...), custom_call_target="tpu_custom_call" | custom-call | flops 2621440 | bytes 4194304 | tf_op jit(solution)/shard_map/pallas_call | solution.py:296
  6.9 1.6 %collective-permute-start = (f32[2,16,16,128]{3,2,1,0:T(8,128)S(1)}, f32[2,16,16,128]{3,2,1,0:T(8,128)S(1)}, u32[]{:S(2)}, u32[]{:S(2)}) collective-permute-start(f32[2,16,16,128]{3,2,1,0:T(8,128)S(1)} %get-tuple-element.28), channel_id=1, source_target_pairs={{0,4},{4,0},{8,12},{12,8},{16,20},{20,16},{24,28},{28,24},{32,36},... | collective-permute-start | bytes 786440 | tf_op jit(solution)/shard_map/ppermute | solution.py:311
  8.5 9.0 %collective-permute-start.1 = (f32[2,16,16,128]{3,2,1,0:T(8,128)S(1)}, f32[2,16,16,128]{3,2,1,0:T(8,128)S(1)}, u32[]{:S(2)}, u32[]{:S(2)}) collective-permute-start(f32[2,16,16,128]{3,2,1,0:T(8,128)S(1)} %get-tuple-element.29), channel_id=1, source_target_pairs={{4,8},{8,4},{12,16},{16,12},{20,24},{24,20},{28,32},{32,28},{36,40... | collective-permute-start | bytes 786440 | tf_op jit(solution)/shard_map/ppermute | solution.py:311
  17.5 0.1 collective-permute-start.2
  17.6 3.0 %collective-permute-start.3 = (f32[16,128]{1,0:T(8,128)S(1)}, f32[16,128]{1,0:T(8,128)S(1)}, u32[]{:S(2)}, u32[]{:S(2)}) collective-permute-start(f32[16,128]{1,0:T(8,128)S(1)} %get-tuple-element.31), channel_id=1, source_target_pairs={{1,2},{2,1},{5,6},{6,5},{9,10},{10,9},{13,14},{14,13},{17,18},{18,... | collective-permute-start | bytes 24584 | tf_op jit(solution)/shard_map/ppermute | solution.py:311
  20.7 6.5 %collective-permute-done.3.r2 = f32[16,128]{1,0:T(8,128)S(1)} collective-permute-done((f32[16,128]{1,0:T(8,128)S(1)}, f32[16,128]{1,0:T(8,128)S(1)}, u32[]{:S(2)}, u32[]{:S(2)}) %collective-permute-start.3) | collective-permute-done | bytes 8224 | tf_op jit(solution)/shard_map/ppermute | solution.py:311
  27.2 1.9 %collective-permute-start.5 = (f32[2,16,128]{2,1,0:T(8,128)S(1)}, f32[2,16,128]{2,1,0:T(8,128)S(1)}, u32[]{:S(2)}, u32[]{:S(2)}) collective-permute-start(f32[2,16,128]{2,1,0:T(8,128)S(1)} %pad_maximum_fusion), channel_id=1, source_target_pairs={{4,8},{8,4},{12,16},{16,12},{20,24},{24,20},{28,32},{32,28},{36,40... | collective-permute-start | bytes 49160 | tf_op jit(solution)/shard_map/ppermute | solution.py:311
  29.2 8.7 %collective-permute-done.5.cb = f32[2,16,128]{2,1,0:T(8,128)S(1)} collective-permute-done((f32[2,16,128]{2,1,0:T(8,128)S(1)}, f32[2,16,128]{2,1,0:T(8,128)S(1)}, u32[]{:S(2)}, u32[]{:S(2)}) %collective-permute-start.5) | collective-permute-done | bytes 16416 | tf_op jit(solution)/shard_map/ppermute | solution.py:311
  37.9 1.7 %shard_map.94 = (f32[2,16,16,128]{3,2,1,0:T(8,128)S(1)}, f32[2,16,16,128]{3,2,1,0:T(8,128)S(1)}, f32[16,128]{1,0:T(8,128)S(1)}, f32[16,128]{1,0:T(8,128)S(1)}, f...) custom-call(f32[2,16,16,128]{3,2,1,0:T(8,128)S(1)} %copy-done.4, ...), custom_call_target="tpu_custom_call" | custom-call | flops 5242880 | bytes 4194304 | tf_op jit(solution)/shard_map/pallas_call | solution.py:296
  39.6 0.1 collective-permute-start.6
  39.7 4.2 %collective-permute-start.7 = (f32[2,16,16,128]{3,2,1,0:T(8,128)S(1)}, f32[2,16,16,128]{3,2,1,0:T(8,128)S(1)}, u32[]{:S(2)}, u32[]{:S(2)}) collective-permute-start(f32[2,16,16,128]{3,2,1,0:T(8,128)S(1)} %get-tuple-element.41), channel_id=1, source_target_pairs={{4,8},{8,4},{12,16},{16,12},{20,24},{24,20},{28,32},{32,28},{36,40... | collective-permute-start | bytes 786440 | tf_op jit(solution)/shard_map/ppermute | solution.py:311
  43.9 0.1 collective-permute-start.8
  44.0 1.9 %collective-permute-start.9 = (f32[16,128]{1,0:T(8,128)S(1)}, f32[16,128]{1,0:T(8,128)S(1)}, u32[]{:S(2)}, u32[]{:S(2)}) collective-permute-start(f32[16,128]{1,0:T(8,128)S(1)} %get-tuple-element.43), channel_id=1, source_target_pairs={{1,2},{2,1},{5,6},{6,5},{9,10},{10,9},{13,14},{14,13},{17,18},{18,... | collective-permute-start | bytes 24584 | tf_op jit(solution)/shard_map/ppermute | solution.py:311
  46.0 3.0 %collective-permute-done.9.r2 = f32[16,128]{1,0:T(8,128)S(1)} collective-permute-done((f32[16,128]{1,0:T(8,128)S(1)}, f32[16,128]{1,0:T(8,128)S(1)}, u32[]{:S(2)}, u32[]{:S(2)}) %collective-permute-start.9) | collective-permute-done | bytes 8224 | tf_op jit(solution)/shard_map/ppermute | solution.py:311
  49.0 9.3 %collective-permute-start.11 = (f32[2,16,128]{2,1,0:T(8,128)S(1)}, f32[2,16,128]{2,1,0:T(8,128)S(1)}, u32[]{:S(2)}, u32[]{:S(2)}) collective-permute-start(f32[2,16,128]{2,1,0:T(8,128)S(1)} %pad_maximum_fusion.1), channel_id=1, source_target_pairs={{4,8},{8,4},{12,16},{16,12},{20,24},{24,20},{28,32},{32,28},{36,40... | collective-permute-start | bytes 49160 | tf_op jit(solution)/shard_map/ppermute | solution.py:311
  58.3 0.1 collective-permute-start.10
  58.4 1.6 %shard_map.95 = (f32[2,16,16,128]{3,2,1,0:T(8,128)}, f32[2,16,16,128]{3,2,1,0:T(8,128)S(1)}, f32[4,2,16,16,128]{4,3,2,1,0:T(8,128)S(1)}, f32[6,2,16,16,128]{4,3,2,1,0:T(8,128)S(1)}) custom-call(f32[2,16,16,128]{3,2,1,0:T(8,128)S(1)} %copy-done.4, s32[2,16,16,128]{3,2,1,0:T(8,128)S(1)} %bitcast.7, f32[4,2,16,16,128]{4,3,2,1,0:T(8,128)S(1)} %copy-done.2, ...), custom_call_target="tpu_custom_call" | custom-call | flops 3932160 | bytes 4194304 | tf_op jit(solution)/shard_map/pallas_call | solution.py:296
  60.0 2.1 %collective-permute-done.10.ca = f32[2,16,128]{2,1,0:T(8,128)S(1)} collective-permute-done((f32[2,16,128]{2,1,0:T(8,128)S(1)}, f32[2,16,128]{2,1,0:T(8,128)S(1)}, u32[]{:S(2)}, u32[]{:S(2)}) %collective-permute-start.10) | collective-permute-done | bytes 16416 | tf_op jit(solution)/shard_map/ppermute | solution.py:311
  62.1 2.6 %shard_map.96 = (f32[2,16,16,128]{3,2,1,0:T(8,128)}, f32[4,2,16,16,128]{4,3,2,1,0:T(8,128)}, f32[6,2,16,16,128]{4,3,2,1,0:T(8,128)}) custom-call(f32[2,16,16,128]{3,2,1,0:T(8,128)S(1)} %copy-done.4, f32[2,16,16,128]{3,2,1,0:T(8,128)S(1)} %get-tuple-element.32.u1, f32[4,2,16,16,128]{4,3,2,1,0:T(8,128)S(1)} %copy-done.2, f32[6,2,16,16,128]{4,3,2,1,0:T(8,128)S(1)} %copy-done.1, ...), custom_call_target="tpu_custom_call" | custom-call | flops 3932160 | bytes 4194304 | tf_op jit(solution)/shard_map/pallas_call | solution.py:296
  (22 shorter events, 0.2 us)
Async XLA Ops:
  0.6 1.4 %copy-start = (f32[6,2,16,16,128]{4,3,2,1,0:T(8,128)S(1)}, f32[6,2,16,16,128]{4,3,2,1,0:T(8,128)}, u32[]{:S(2)}) copy-start(f32[6,2,16,16,128]{4,3,2,1,0:T(8,128)} %crs.7) | copy-start | bytes 4718596
  2.0 1.2 %copy-start.2 = (f32[4,2,16,16,128]{4,3,2,1,0:T(8,128)S(1)}, f32[4,2,16,16,128]{4,3,2,1,0:T(8,128)}, u32[]{:S(2)}) copy-start(f32[4,2,16,16,128]{4,3,2,1,0:T(8,128)} %dif.7) | copy-start | bytes 3145732
  3.3 0.9 %copy-start.3 = (f32[2,16,16,128]{3,2,1,0:T(8,128)S(1)}, f32[2,16,16,128]{3,2,1,0:T(8,128)}, u32[]{:S(2)}) copy-start(f32[2,16,16,128]{3,2,1,0:T(8,128)} %val.7) | copy-start | bytes 786436
  4.2 0.9 %copy-start.5 = (s32[1,2,16,16,128]{4,3,2,1,0:T(8,128)S(1)}, s32[1,2,16,16,128]{4,3,2,1,0:T(8,128)}, u32[]{:S(2)}) copy-start(s32[1,2,16,16,128]{4,3,2,1,0:T(8,128)} %param.10) | copy-start | bytes 786436
  5.2 0.9 %copy-start.6 = (f32[2,16,16,128]{3,2,1,0:T(8,128)S(1)}, f32[2,16,16,128]{3,2,1,0:T(8,128)}, u32[]{:S(2)}) copy-start(f32[2,16,16,128]{3,2,1,0:T(8,128)} %cot.3) | copy-start | bytes 786436
  6.1 31.8 %copy-start.1 = (f32[6,2,16,16,128]{4,3,2,1,0:T(8,128)S(1)}, f32[6,2,16,16,128]{4,3,2,1,0:T(8,128)}, u32[]{:S(2)}) copy-start(f32[6,2,16,16,128]{4,3,2,1,0:T(8,128)} %crs.7) | copy-start | bytes 4718596
  6.1 31.8 %copy-start.4 = (f32[2,16,16,128]{3,2,1,0:T(8,128)S(1)}, f32[2,16,16,128]{3,2,1,0:T(8,128)}, u32[]{:S(2)}) copy-start(f32[2,16,16,128]{3,2,1,0:T(8,128)} %val.7) | copy-start | bytes 786436
  6.1 31.8 %copy-start.7 = (f32[2,16,16,128]{3,2,1,0:T(8,128)S(1)}, f32[2,16,16,128]{3,2,1,0:T(8,128)}, u32[]{:S(2)}) copy-start(f32[2,16,16,128]{3,2,1,0:T(8,128)} %pay.1) | copy-start | bytes 786436
  6.9 31.0 %collective-permute-start = (f32[2,16,16,128]{3,2,1,0:T(8,128)S(1)}, f32[2,16,16,128]{3,2,1,0:T(8,128)S(1)}, u32[]{:S(2)}, u32[]{:S(2)}) collective-permute-start(f32[2,16,16,128]{3,2,1,0:T(8,128)S(1)} %get-tuple-element.28), channel_id=1, source_target_pairs={{0,4},{4,0},{8,12},{12,8},{16,20},{20,16},{24,28},{28,24},{32,36},... | collective-permute-start | bytes 786440 | tf_op jit(solution)/shard_map/ppermute | solution.py:311
  8.5 29.4 %collective-permute-start.1 = (f32[2,16,16,128]{3,2,1,0:T(8,128)S(1)}, f32[2,16,16,128]{3,2,1,0:T(8,128)S(1)}, u32[]{:S(2)}, u32[]{:S(2)}) collective-permute-start(f32[2,16,16,128]{3,2,1,0:T(8,128)S(1)} %get-tuple-element.29), channel_id=1, source_target_pairs={{4,8},{8,4},{12,16},{16,12},{20,24},{24,20},{28,32},{32,28},{36,40... | collective-permute-start | bytes 786440 | tf_op jit(solution)/shard_map/ppermute | solution.py:311
  17.5 3.1 %collective-permute-start.2 = (f32[16,128]{1,0:T(8,128)S(1)}, f32[16,128]{1,0:T(8,128)S(1)}, u32[]{:S(2)}, u32[]{:S(2)}) collective-permute-start(f32[16,128]{1,0:T(8,128)S(1)} %get-tuple-element.30), channel_id=1, source_target_pairs={{0,1},{1,0},{2,3},{3,2},{4,5},{5,4},{6,7},{7,6},{8,9},{9,8},{10,11... | collective-permute-start | bytes 24584 | tf_op jit(solution)/shard_map/ppermute | solution.py:311
  17.6 9.5 %collective-permute-start.3 = (f32[16,128]{1,0:T(8,128)S(1)}, f32[16,128]{1,0:T(8,128)S(1)}, u32[]{:S(2)}, u32[]{:S(2)}) collective-permute-start(f32[16,128]{1,0:T(8,128)S(1)} %get-tuple-element.31), channel_id=1, source_target_pairs={{1,2},{2,1},{5,6},{6,5},{9,10},{10,9},{13,14},{14,13},{17,18},{18,... | collective-permute-start | bytes 24584 | tf_op jit(solution)/shard_map/ppermute | solution.py:311
  27.2 10.7 %collective-permute-start.5 = (f32[2,16,128]{2,1,0:T(8,128)S(1)}, f32[2,16,128]{2,1,0:T(8,128)S(1)}, u32[]{:S(2)}, u32[]{:S(2)}) collective-permute-start(f32[2,16,128]{2,1,0:T(8,128)S(1)} %pad_maximum_fusion), channel_id=1, source_target_pairs={{4,8},{8,4},{12,16},{16,12},{20,24},{24,20},{28,32},{32,28},{36,40... | collective-permute-start | bytes 49160 | tf_op jit(solution)/shard_map/ppermute | solution.py:311
  29.1 8.8 %collective-permute-start.4 = (f32[2,16,128]{2,1,0:T(8,128)S(1)}, f32[2,16,128]{2,1,0:T(8,128)S(1)}, u32[]{:S(2)}, u32[]{:S(2)}) collective-permute-start(f32[2,16,128]{2,1,0:T(8,128)S(1)} %pad_maximum_fusion), channel_id=1, source_target_pairs={{0,4},{4,0},{8,12},{12,8},{16,20},{20,16},{24,28},{28,24},{32,36},... | collective-permute-start | bytes 49160 | tf_op jit(solution)/shard_map/ppermute | solution.py:311
  39.6 22.5 %collective-permute-start.6 = (f32[2,16,16,128]{3,2,1,0:T(8,128)S(1)}, f32[2,16,16,128]{3,2,1,0:T(8,128)S(1)}, u32[]{:S(2)}, u32[]{:S(2)}) collective-permute-start(f32[2,16,16,128]{3,2,1,0:T(8,128)S(1)} %get-tuple-element.40), channel_id=1, source_target_pairs={{0,4},{4,0},{8,12},{12,8},{16,20},{20,16},{24,28},{28,24},{32,36},... | collective-permute-start | bytes 786440 | tf_op jit(solution)/shard_map/ppermute | solution.py:311
  39.7 22.4 %collective-permute-start.7 = (f32[2,16,16,128]{3,2,1,0:T(8,128)S(1)}, f32[2,16,16,128]{3,2,1,0:T(8,128)S(1)}, u32[]{:S(2)}, u32[]{:S(2)}) collective-permute-start(f32[2,16,16,128]{3,2,1,0:T(8,128)S(1)} %get-tuple-element.41), channel_id=1, source_target_pairs={{4,8},{8,4},{12,16},{16,12},{20,24},{24,20},{28,32},{32,28},{36,40... | collective-permute-start | bytes 786440 | tf_op jit(solution)/shard_map/ppermute | solution.py:311
  43.9 2.0 %collective-permute-start.8 = (f32[16,128]{1,0:T(8,128)S(1)}, f32[16,128]{1,0:T(8,128)S(1)}, u32[]{:S(2)}, u32[]{:S(2)}) collective-permute-start(f32[16,128]{1,0:T(8,128)S(1)} %get-tuple-element.42), channel_id=1, source_target_pairs={{0,1},{1,0},{2,3},{3,2},{4,5},{5,4},{6,7},{7,6},{8,9},{9,8},{10,11... | collective-permute-start | bytes 24584 | tf_op jit(solution)/shard_map/ppermute | solution.py:311
  44.0 5.0 %collective-permute-start.9 = (f32[16,128]{1,0:T(8,128)S(1)}, f32[16,128]{1,0:T(8,128)S(1)}, u32[]{:S(2)}, u32[]{:S(2)}) collective-permute-start(f32[16,128]{1,0:T(8,128)S(1)} %get-tuple-element.43), channel_id=1, source_target_pairs={{1,2},{2,1},{5,6},{6,5},{9,10},{10,9},{13,14},{14,13},{17,18},{18,... | collective-permute-start | bytes 24584 | tf_op jit(solution)/shard_map/ppermute | solution.py:311
  49.0 11.0 %collective-permute-start.11 = (f32[2,16,128]{2,1,0:T(8,128)S(1)}, f32[2,16,128]{2,1,0:T(8,128)S(1)}, u32[]{:S(2)}, u32[]{:S(2)}) collective-permute-start(f32[2,16,128]{2,1,0:T(8,128)S(1)} %pad_maximum_fusion.1), channel_id=1, source_target_pairs={{4,8},{8,4},{12,16},{16,12},{20,24},{24,20},{28,32},{32,28},{36,40... | collective-permute-start | bytes 49160 | tf_op jit(solution)/shard_map/ppermute | solution.py:311
  58.3 3.8 %collective-permute-start.10 = (f32[2,16,128]{2,1,0:T(8,128)S(1)}, f32[2,16,128]{2,1,0:T(8,128)S(1)}, u32[]{:S(2)}, u32[]{:S(2)}) collective-permute-start(f32[2,16,128]{2,1,0:T(8,128)S(1)} %pad_maximum_fusion.1), channel_id=1, source_target_pairs={{0,4},{4,0},{8,12},{12,8},{16,20},{20,16},{24,28},{28,24},{32,36},... | collective-permute-start | bytes 49160 | tf_op jit(solution)/shard_map/ppermute | solution.py:311

commit v2 on v1

v2 whole, which is shorter than its diff:
```python
import jax
import jax.numpy as jnp
from jax import lax
from jax.experimental import pallas as pl
from jax.experimental.pallas import tpu as pltpu
from jax.sharding import PartitionSpec as P

F32 = jnp.float32
TILE = (16, 128)
BLOCK = (2, 16, 16, 128)
CHUNK = 4
CHUNKS = 16 // CHUNK


def lanes():
    return lax.broadcasted_iota(jnp.int32, TILE, 1)


def rows():
    return lax.broadcasted_iota(jnp.int32, TILE, 0)


def lane_roll(x, shift):
    shift = shift % 128
    return x if shift == 0 else pltpu.roll(x, shift, 1)


def up2(x, row):
    return jnp.where(row == 15, 0.0, pltpu.roll(x, 15, 0))


def down2(x, row):
    return jnp.where(row == 0, 0.0, pltpu.roll(x, 1, 0))


def both(ref, r, i):
    if i == 0:
        return ref[r, 1], ref[r, 1]
    if i == 15:
        return ref[r, 14], -ref[r, 14]
    return ref[r, i + 1] + ref[r, i - 1], ref[r, i + 1] - ref[r, i - 1]


def wide_odd():
    return lax.rem(lax.axis_index("wide"), 2)


def narrow_odd():
    return lax.rem(lax.axis_index("narrow"), 2)


def narrow_sides(first, second):
    even = narrow_odd() == 0
    return jnp.where(even, first, second), jnp.where(even, second, first)


def corner_sides(cor_a, cor_b):
    even = wide_odd() == 0
    a_right, a_left = narrow_sides(cor_a[0], cor_a[1])
    b_right, b_left = narrow_sides(cor_b[0], cor_b[1])
    low = jnp.where(even, b_right, a_right), jnp.where(even, b_left, a_left)
    high = jnp.where(even, a_right, b_right), jnp.where(even, a_left, b_left)
    return low, high


def from_wide(ra, rb, part, r, i):
    even = wide_odd() == 0
    low, high = (rb, ra) if r == 0 else (ra, rb)
    return jnp.where(even, low[part, i], high[part, i])


def adjoint(w_of, u_of, dif, crs, scratch, msg_a, msg_b, n1, n2, adj_of):
    q1s, p01s, p12s, p13s, x2s, y2s, x3s, y3s, q0s, p02s, p03s = scratch
    row, lane = rows(), lanes()
    for i in range(16):
        w = [w_of(r, i) for r in range(2)]
        h = [0.25 * w[r] for r in range(2)]
        p02 = [crs[1, r, i] * h[r] for r in range(2)]
        p03 = [crs[2, r, i] * h[r] for r in range(2)]
        for r in range(2):
            q0s[r, i] = dif[0, r, i] * w[r]
            q1s[r, i] = dif[1, r, i] * w[r]
            p01s[r, i] = crs[0, r, i] * h[r]
            p12s[r, i] = crs[3, r, i] * h[r]
            p13s[r, i] = crs[4, r, i] * h[r]
            p02s[r, i] = p02[r]
            p03s[r, i] = p03[r]
            q2 = dif[2, r, i] * w[r]
            e02 = p02[1] if r == 0 else -p02[0]
            x2s[r, i] = q2 + e02
            y2s[r, i] = q2 - e02
            q3 = dif[3, r, i] * w[r]
            p23 = crs[5, r, i] * h[r]
            e3 = (p03[1] if r == 0 else -p03[0]) + (up2(p23, row) - down2(p23, row))
            x3s[r, i] = q3 + e3
            y3s[r, i] = q3 - e3
    odd = wide_odd()
    row_a = 1 - odd
    row_b = odd
    sign_a = (2 * odd - 1).astype(F32)
    left = jnp.zeros(TILE, F32)
    right = jnp.zeros(TILE, F32)

    def put(packed, value, source, column):
        return jnp.where(lane == column, lane_roll(value, column - source), packed)

    for i in range(16):
        for r in range(2):
            u = u_of(r, i)
            left = put(left, u, 0, r * 16 + i)
            right = put(right, u, 127, r * 16 + i)
            f12 = both(p12s, r, i)[1]
            f13 = both(p13s, r, i)[1]
            x3 = x3s[r, i] + f13
            y3 = y3s[r, i] - f13
            x2 = x2s[r, i] + f12
            y2 = y2s[r, i] - f12
            e01 = both(p01s, 1 - r, i)[1]
            total = q0s[1 - r, i] + both(q1s, r, i)[0]
            total = total + e01 if r == 0 else total - e01
            total = total + up2(x2, row) + down2(y2, row)
            total = total + jnp.where(lane == 127, 0.0, lane_roll(x3, 127)) + jnp.where(lane == 0, 0.0, lane_roll(y3, 1))
            adj_of(r, i, total)
            left = put(left, x3, 0, 48 + r * 16 + i)
            right = put(right, y3, 127, 48 + r * 16 + i)
        p0, p1 = p03s[0, i], p03s[1, i]
        left = put(left, p0, 0, 32 + i)
        right = put(right, -p0, 127, 32 + i)
        left = put(left, -p1, 0, 80 + i)
        right = put(right, p1, 127, 80 + i)
        for msg, at, sign in ((msg_a, row_a, sign_a), (msg_b, row_b, -sign_a)):
            p02, p03 = p02s[at, i], p03s[at, i]
            d = both(p01s, at, i)[1]
            d = d + up2(p02, row) - down2(p02, row)
            d = d + jnp.where(lane == 127, 0.0, lane_roll(p03, 127)) - jnp.where(lane == 0, 0.0, lane_roll(p03, 1))
            msg[1, i] = q0s[at, i] + sign * d
            msg[0, i] = u_of(at, i)
    even = narrow_odd() == 0
    n1[...] = jnp.where(even, right, left)
    n2[...] = jnp.where(even, left, right)


def inner(us, r1, r2, scratch):
    d2s, d3s, n2s, n3s = scratch
    row, lane = rows(), lanes()
    from_right, from_left = narrow_sides(r1[...], r2[...])
    for i in range(16):
        for r in range(2):
            x = us[r, i]
            at = r * 16 + i
            plus = jnp.where(lane == 127, lane_roll(from_right, 127 - at), lane_roll(x, 127))
            minus = jnp.where(lane == 0, lane_roll(from_left, -at), lane_roll(x, 1))
            above, below = up2(x, row), down2(x, row)
            d3s[r, i] = plus - minus
            d2s[r, i] = above - below
            n3s[r, i] = plus + minus
            n2s[r, i] = above + below

    def at(r, i):
        d3 = d3s[r, i]
        sign = 0.25 if r == 0 else -0.25
        sums = (us[1 - r, i], both(us, r, i)[0], n2s[r, i], n3s[r, i])
        mixed = (
            sign * both(us, 1 - r, i)[1],
            sign * d2s[1 - r, i],
            sign * d3s[1 - r, i],
            0.25 * both(d2s, r, i)[1],
            0.25 * both(d3s, r, i)[1],
            0.25 * (up2(d3, row) - down2(d3, row)),
        )
        return sums, mixed

    return at


def outer(ra, rb, ca, cb):
    row, lane = rows(), lanes()
    low, high = corner_sides(ca, cb)

    def at(r, i):
        x = from_wide(ra, rb, 0, r, i)
        (pack_right, pack_left), base = (low, 16) if r == 0 else (high, 0)
        sign = -0.25 if r == 0 else 0.25
        if i == 0:
            d1 = from_wide(ra, rb, 0, r, 1)
        elif i == 15:
            d1 = -from_wide(ra, rb, 0, r, 14)
        else:
            d1 = from_wide(ra, rb, 0, r, i + 1) - from_wide(ra, rb, 0, r, i - 1)
        d2 = up2(x, row) - down2(x, row)
        plus = jnp.where(lane == 127, lane_roll(pack_right, 127 - base - i), lane_roll(x, 127))
        minus = jnp.where(lane == 0, lane_roll(pack_left, -base - i), lane_roll(x, 1))
        return x, (sign * d1, sign * d2, sign * (plus - minus))

    return at


def columns(right, left):
    lane = lanes()

    def at(r, i):
        k = r * 16 + i
        return jnp.where(lane == 127, lane_roll(right, 127 - k), jnp.where(lane == 0, lane_roll(left, -k), 0.0))

    return at


def narrow_overhang(r1, r2):
    right, left = narrow_sides(r1[...], r2[...])
    return columns(lane_roll(right, -48), lane_roll(left, -48))


def corner_overhang(ca, cb):
    lane = lanes()
    low, high = corner_sides(ca, cb)
    merged = [jnp.where(lane < 16, lane_roll(low[k], -80), lane_roll(high[k], -16)) for k in range(2)]
    return columns(*merged)


ADJOINT_SCRATCH = [pltpu.VMEM(BLOCK, F32)] * 11
INNER_SCRATCH = [pltpu.VMEM(BLOCK, F32)] * 4


def kernel_a(cot_h, flg_h, dif_h, crs_h, val_h, msg_a, msg_b, n1, n2, inv, w2, adj, cot, flg, val, dif, crs, sems, *scratch):
    copies = []
    for c in range(CHUNKS):
        span = pl.ds(c * CHUNK, CHUNK)
        group = []
        for k, (src, dst) in enumerate(((cot_h, cot), (flg_h, flg), (val_h, val))):
            group.append(pltpu.make_async_copy(src.at[:, span], dst.at[:, span], sems.at[c, k]))
        for k, (src, dst) in enumerate(((dif_h, dif), (crs_h, crs))):
            group.append(pltpu.make_async_copy(src.at[:, :, span], dst.at[:, :, span], sems.at[c, 3 + k]))
        for copy in group:
            copy.start()
        copies.append(group)

    def weight(r, i):
        if r == 0 and i % CHUNK == 0:
            for copy in copies[i // CHUNK]:
                copy.wait()
        recip = 1.0 / (1.0 + 2.0 * (dif[0, r, i] + dif[1, r, i] + dif[2, r, i] + dif[3, r, i]))
        inv[r, i] = recip
        w = jnp.where(flg[r, i] == 1, 0.0, cot[r, i] * recip)
        w2[r, i] = w
        return w

    def keep(r, i, total):
        adj[r, i] = total

    adjoint(weight, lambda r, i: val[r, i], dif, crs, scratch, msg_a, msg_b, n1, n2, keep)


def kernel_p(val, dif, crs, adj_in, r1, r2, total, adj, *scratch):
    at = inner(val, r1, r2, scratch)
    column = narrow_overhang(r1, r2)
    for i in range(16):
        for r in range(2):
            sums, mixed = at(r, i)
            value = val[r, i]
            for k in range(4):
                value = value + dif[k, r, i] * sums[k]
            for k in range(6):
                value = value + crs[k, r, i] * mixed[k]
            total[r, i] = value
            adj[r, i] = adj_in[r, i] + column(r, i)


def kernel_b(pay, flg, dif, crs, inv, total, adj_in, ra, rb, ca, cb, msg_a, msg_b, n1, n2, u1, w1, adj1, adj0, *scratch):
    beyond = outer(ra, rb, ca, cb)
    column = corner_overhang(ca, cb)

    def weight(r, i):
        x, mixed = beyond(r, i)
        value = total[r, i] + dif[0, r, i] * x
        for k in range(3):
            value = value + crs[k, r, i] * mixed[k]
        exercised = flg[r, i] == 1
        recip = inv[r, i]
        u1[r, i] = jnp.where(exercised, pay[r, i], value * recip)
        adjoint_value = adj_in[r, i] + from_wide(ra, rb, 1, r, i) + column(r, i)
        adj1[r, i] = adjoint_value
        w = jnp.where(exercised, 0.0, adjoint_value * recip)
        w1[r, i] = w
        return w

    def keep(r, i, value):
        adj0[r, i] = value

    adjoint(weight, lambda r, i: u1[r, i], dif, crs, scratch, msg_a, msg_b, n1, n2, keep)


def kernel_m(
    val, u1, flg, dif, crs, inv, total, w1, w2, cot, adj1, adj0, ra, rb, r1, r2, ca, cb, s1, s2,
    gpay, gc, part, pd, pc, out_pay, out_gc, sems, *scratch,
):
    first = inner(val, r1, r2, scratch[:4])
    beyond = outer(ra, rb, ca, cb)
    second = inner(u1, s1, s2, scratch[4:])
    column = narrow_overhang(s1, s2)
    for i in range(16):
        for r in range(2):
            sums, mixed = first(r, i)
            x, more = beyond(r, i)
            sums = (sums[0] + x, *sums[1:])
            value = total[r, i] + dif[0, r, i] * x
            for k in range(3):
                value = value + crs[k, r, i] * more[k]
            mixed = (*(mixed[k] + more[k] for k in range(3)), *mixed[3:])
            sums_2, mixed_2 = second(r, i)
            value_2 = val[r, i]
            for k in range(4):
                value_2 = value_2 + dif[k, r, i] * sums_2[k]
            for k in range(6):
                value_2 = value_2 + crs[k, r, i] * mixed_2[k]
            recip = 2.0 * inv[r, i]
            twice, twice_2 = value * recip, value_2 * recip
            w, v = w1[r, i], w2[r, i]
            for k in range(4):
                pd[k, r, i] = w * (sums[k] - twice) + v * (sums_2[k] - twice_2)
            for k in range(3):
                pc[k, r, i] = w * mixed[k] + v * mixed_2[k]
            for k in range(3, 6):
                out_gc[k - 3, r, i] = w * mixed[k] + v * mixed_2[k]
            out_pay[r, i] = jnp.where(flg[r, i] == 1, cot[r, i] + adj1[r, i], 0.0)
            part[r, i] = adj0[r, i] + w + v + column(r, i)
    copies = [pltpu.make_async_copy(out_pay, gpay, sems.at[0]), pltpu.make_async_copy(out_gc, gc.at[pl.ds(3, 3)], sems.at[1])]
    for copy in copies:
        copy.start()
    for copy in copies:
        copy.wait()


def kernel_c(dif, crs, inv, w2, part, pd, pc, ra, rb, ca, cb, gc_in, gval, gd, gc, out_val, out_d, out_c, sems):
    del gc_in
    beyond = outer(ra, rb, ca, cb)
    column = corner_overhang(ca, cb)
    copies = []
    for i in range(16):
        for r in range(2):
            x, more = beyond(r, i)
            value = dif[0, r, i] * x
            for k in range(3):
                value = value + crs[k, r, i] * more[k]
            v = w2[r, i]
            change = (2.0 * inv[r, i]) * v * value
            out_d[0, r, i] = pd[0, r, i] + (v * x - change)
            for k in range(1, 4):
                out_d[k, r, i] = pd[k, r, i] - change
            for k in range(3):
                out_c[k, r, i] = pc[k, r, i] + v * more[k]
            out_val[r, i] = part[r, i] + from_wide(ra, rb, 1, r, i) + column(r, i)
        if i % CHUNK == CHUNK - 1:
            c = i // CHUNK
            span = pl.ds(c * CHUNK, CHUNK)
            group = [
                pltpu.make_async_copy(out_d.at[:, :, span], gd.at[:, :, span], sems.at[c, 0]),
                pltpu.make_async_copy(out_c.at[:, :, span], gc.at[pl.ds(0, 3), :, span], sems.at[c, 1]),
                pltpu.make_async_copy(out_val.at[:, span], gval.at[:, span], sems.at[c, 2]),
            ]
            for copy in group:
                copy.start()
            copies += group
    for copy in copies:
        copy.wait()


V = pltpu.VMEM
H = pltpu.HBM


def call(kernel, outs, scratch, flops, args, spaces=None, aliases=None, limit=160):
    return pl.pallas_call(
        kernel,
        out_shape=[jax.ShapeDtypeStruct(out[0], out[2] if len(out) > 2 else F32) for out in outs],
        in_specs=[pl.BlockSpec(memory_space=space) for space in (spaces or [V] * len(args))],
        out_specs=[pl.BlockSpec(memory_space=out[1]) for out in outs],
        scratch_shapes=scratch,
        input_output_aliases=aliases or {},
        cost_estimate=pl.CostEstimate(flops=flops, bytes_accessed=4 << 20, transcendentals=0),
        compiler_params=pltpu.CompilerParams(vmem_limit_bytes=limit << 18),
    )(*args)


def swap(x, axis, odd):
    pairs = []
    for i in range(odd, lax.axis_size(axis) - 1, 2):
        pairs += [(i, i + 1), (i + 1, i)]
    return lax.ppermute(x, axis, pairs)


def exchange(msg_a, msg_b, n1, n2):
    r2 = swap(n2, "narrow", 1)
    rb = swap(msg_b, "wide", 1)
    r1 = swap(n1, "narrow", 0)
    ra = swap(msg_a, "wide", 0)
    corners = jnp.stack([r1, r2])
    cb = swap(corners, "wide", 1)
    ca = swap(corners, "wide", 0)
    return ra, rb, r1, r2, ca, cb


def body(value_in, payoff, diffusion, cross_terms, flags, cotangent):
    four, six = (4, *BLOCK), (6, *BLOCK)
    message = (2, 16, *TILE)
    sends = [(message, V), (message, V), (TILE, V), (TILE, V)]
    block = (BLOCK, V)
    msg_a, msg_b, n1, n2, inv, w2, adj, cot, flg, val = call(
        kernel_a,
        [*sends, block, block, block, block, (BLOCK, V, jnp.int32), block],
        [pltpu.VMEM(four, F32), pltpu.VMEM(six, F32), pltpu.SemaphoreType.DMA((CHUNKS, 5)), *ADJOINT_SCRATCH],
        40 << 16,
        (cotangent, flags[0], diffusion, cross_terms, value_in),
        [H] * 5,
        limit=207,
    )
    ra, rb, r1, r2, ca, cb = exchange(msg_a, msg_b, n1, n2)
    total, adj = call(kernel_p, [block, block], INNER_SCRATCH, 40 << 16, (val, diffusion, cross_terms, adj, r1, r2))
    msg_a, msg_b, n1, n2, u1, w1, adj1, adj0 = call(
        kernel_b,
        [*sends, block, block, block, block],
        ADJOINT_SCRATCH,
        60 << 16,
        (payoff, flg, diffusion, cross_terms, inv, total, adj, ra, rb, ca, cb),
    )
    sa, sb, s1, s2, da, db = exchange(msg_a, msg_b, n1, n2)
    gpay, gc, part, pd, pc = call(
        kernel_m,
        [(BLOCK, H), (six, H), block, (four, V), ((3, *BLOCK), V)],
        [pltpu.VMEM(BLOCK, F32), pltpu.VMEM((3, *BLOCK), F32), pltpu.SemaphoreType.DMA((2,)), *INNER_SCRATCH, *INNER_SCRATCH],
        120 << 16,
        (val, u1, flg, diffusion, cross_terms, inv, total, w1, w2, cot, adj1, adj0, ra, rb, r1, r2, ca, cb, s1, s2),
    )
    gval, gd, gc = call(
        kernel_c,
        [(BLOCK, H), (four, H), (six, H)],
        [pltpu.VMEM(BLOCK, F32), pltpu.VMEM(four, F32), pltpu.VMEM((3, *BLOCK), F32), pltpu.SemaphoreType.DMA((CHUNKS, 3))],
        40 << 16,
        (diffusion, cross_terms, inv, w2, part, pd, pc, sa, sb, da, db, gc),
        [V] * 11 + [H],
        {11: 2},
    )
    return gval, gpay, gd, gc


def solution(mesh):
    field = P("wide", None, None, "narrow")
    stack = P(None, "wide", None, None, "narrow")
    return jax.shard_map(
        body, mesh=mesh, in_specs=(field, field, stack, stack, stack, field), out_specs=(field, field, stack, stack), check_vma=False
    )
```

time: 65.1 us -> 60.4 us (0.928)
  local copies, waits for them, and re-layouts: 5.48 us -> 0.01 us
  Pallas kernels: 6.64 us -> 9.03 us
  waiting for transfers between devices: 20.4 us -> 18.8 us
    unnamed x16 -> x6, local copies, waits for them, and re-layouts: 5.48 us -> 0.01 us
    pallas_call x4 -> x5, Pallas kernels: 6.64 us -> 9.03 us  [call(): pl.pallas_call(kernel, out_shape=[jax.ShapeDtypeStruct(out[0], out[2] if...]
    ppermute x12, waiting for transfers between devices: 20.4 us -> 18.8 us  [swap(): return lax.ppermute(x, axis, pairs)]
  transfers between devices with their start and end apart: 12 -> 12, of which waited for: 4 -> 4; matrix products, arithmetic and copies ran while one was open for 0% -> 0% of each run, Pallas kernels for 2% -> 5%
where the time goes in v2:
time: 60.4 us; the launch traced here: 60.1 us
  starting transfers between devices  31.4 us (52%)
  waiting for transfers between devices  18.8 us (31%)
  Pallas kernels  9.03 us (15%)
  between operations  0.82 us (1%)
    ppermute x12, starting transfers between devices, swap(): return lax.ppermute(x, axis, pairs)  31.4 us
    ppermute x12, waiting for transfers between devices, swap(): return lax.ppermute(x, axis, pairs)  18.8 us
    pallas_call x5, Pallas kernels, call(): pl.pallas_call(kernel, out_shape=[jax.ShapeDtypeStruct(out[0], out[2] if...  9.03 us
  transfers between devices with their start and end apart: 12, of which 4 were waited for; matrix products, arithmetic and copies ran while one was open for 0% of the time, Pallas kernels for 5%

profile of v2, /device:TPU:56, one launch (start us, length us, event | category | flops | bytes accessed | tf_op | source)
XLA Modules:
  0.0 60.1 jit_solution(13158109534168866212)
XLA Ops:
  0.7 3.1 %shard_map.93 = (f32[2,16,16,128]{3,2,1,0:T(8,128)S(1)}, f32[2,16,16,128]{3,2,1,0:T(8,128)S(1)}, f32[16,128]{1,0:T(8,128)S(1)}, f32[16,128]{1,0:T(8,128)S(1)}, f...) custom-call(f32[2,16,16,128]{3,2,1,0:T(8,128)} %cot_h.1, ...), custom_call_target="tpu_custom_call" | custom-call | flops 2621440 | bytes 4194304 | tf_op jit(solution)/shard_map/pallas_call | solution.py:372
  3.7 1.6 %collective-permute-start.2 = (f32[2,16,16,128]{3,2,1,0:T(8,128)S(1)}, f32[2,16,16,128]{3,2,1,0:T(8,128)S(1)}, u32[]{:S(2)}, u32[]{:S(2)}) collective-permute-start(f32[2,16,16,128]{3,2,1,0:T(8,128)S(1)} %get-tuple-element.41), channel_id=1, source_target_pairs={{0,4},{4,0},{8,12},{12,8},{16,20},{20,16},{24,28},{28,24},{32,36},... | collective-permute-start | bytes 786440 | tf_op jit(solution)/shard_map/ppermute | solution.py:388
  5.3 9.0 %collective-permute-start.3 = (f32[2,16,16,128]{3,2,1,0:T(8,128)S(1)}, f32[2,16,16,128]{3,2,1,0:T(8,128)S(1)}, u32[]{:S(2)}, u32[]{:S(2)}) collective-permute-start(f32[2,16,16,128]{3,2,1,0:T(8,128)S(1)} %get-tuple-element.42), channel_id=1, source_target_pairs={{4,8},{8,4},{12,16},{16,12},{20,24},{24,20},{28,32},{32,28},{36,40... | collective-permute-start | bytes 786440 | tf_op jit(solution)/shard_map/ppermute | solution.py:388
  14.3 0.1 collective-permute-start
  14.4 3.0 %collective-permute-start.1 = (f32[16,128]{1,0:T(8,128)S(1)}, f32[16,128]{1,0:T(8,128)S(1)}, u32[]{:S(2)}, u32[]{:S(2)}) collective-permute-start(f32[16,128]{1,0:T(8,128)S(1)} %get-tuple-element.38), channel_id=1, source_target_pairs={{1,2},{2,1},{5,6},{6,5},{9,10},{10,9},{13,14},{14,13},{17,18},{18,... | collective-permute-start | bytes 24584 | tf_op jit(solution)/shard_map/ppermute | solution.py:388
  17.4 0.0 collective-permute-done.r1
  17.4 6.5 %collective-permute-done.1.r2 = f32[16,128]{1,0:T(8,128)S(1)} collective-permute-done((f32[16,128]{1,0:T(8,128)S(1)}, f32[16,128]{1,0:T(8,128)S(1)}, u32[]{:S(2)}, u32[]{:S(2)}) %collective-permute-start.1) | collective-permute-done | bytes 8224 | tf_op jit(solution)/shard_map/ppermute | solution.py:388
  23.9 1.9 %collective-permute-start.5 = (f32[2,16,128]{2,1,0:T(8,128)S(1)}, f32[2,16,128]{2,1,0:T(8,128)S(1)}, u32[]{:S(2)}, u32[]{:S(2)}) collective-permute-start(f32[2,16,128]{2,1,0:T(8,128)S(1)} %pad_maximum_fusion), channel_id=1, source_target_pairs={{4,8},{8,4},{12,16},{16,12},{20,24},{24,20},{28,32},{32,28},{36,40... | collective-permute-start | bytes 49160 | tf_op jit(solution)/shard_map/ppermute | solution.py:388
  25.9 0.1 collective-permute-start.4
  26.0 0.0 copy-start.2
  26.0 0.6 shard_map.94
  26.6 8.1 %collective-permute-done.5.cb = f32[2,16,128]{2,1,0:T(8,128)S(1)} collective-permute-done((f32[2,16,128]{2,1,0:T(8,128)S(1)}, f32[2,16,128]{2,1,0:T(8,128)S(1)}, u32[]{:S(2)}, u32[]{:S(2)}) %collective-permute-start.5) | collective-permute-done | bytes 16416 | tf_op jit(solution)/shard_map/ppermute | solution.py:388
  34.7 0.0 collective-permute-done.4.ca
  34.7 1.3 %shard_map.95 = (f32[2,16,16,128]{3,2,1,0:T(8,128)S(1)}, f32[2,16,16,128]{3,2,1,0:T(8,128)S(1)}, f32[16,128]{1,0:T(8,128)S(1)}, f32[16,128]{1,0:T(8,128)S(1)}, f...) custom-call(f32[2,16,16,128]{3,2,1,0:T(8,128)S(1)} %copy-done.2, ...), custom_call_target="tpu_custom_call" | custom-call | flops 3932160 | bytes 4194304 | tf_op jit(solution)/shard_map/pallas_call | solution.py:372
  36.0 0.1 collective-permute-start.8
  36.1 4.2 %collective-permute-start.9 = (f32[2,16,16,128]{3,2,1,0:T(8,128)S(1)}, f32[2,16,16,128]{3,2,1,0:T(8,128)S(1)}, u32[]{:S(2)}, u32[]{:S(2)}) collective-permute-start(f32[2,16,16,128]{3,2,1,0:T(8,128)S(1)} %get-tuple-element.54), channel_id=1, source_target_pairs={{4,8},{8,4},{12,16},{16,12},{20,24},{24,20},{28,32},{32,28},{36,40... | collective-permute-start | bytes 786440 | tf_op jit(solution)/shard_map/ppermute | solution.py:388
  40.3 0.1 collective-permute-start.6
  40.4 1.9 %collective-permute-start.7 = (f32[16,128]{1,0:T(8,128)S(1)}, f32[16,128]{1,0:T(8,128)S(1)}, u32[]{:S(2)}, u32[]{:S(2)}) collective-permute-start(f32[16,128]{1,0:T(8,128)S(1)} %get-tuple-element.49), channel_id=1, source_target_pairs={{1,2},{2,1},{5,6},{6,5},{9,10},{10,9},{13,14},{14,13},{17,18},{18,... | collective-permute-start | bytes 24584 | tf_op jit(solution)/shard_map/ppermute | solution.py:388
  42.3 3.0 %collective-permute-done.7.s2 = f32[16,128]{1,0:T(8,128)S(1)} collective-permute-done((f32[16,128]{1,0:T(8,128)S(1)}, f32[16,128]{1,0:T(8,128)S(1)}, u32[]{:S(2)}, u32[]{:S(2)}) %collective-permute-start.7) | collective-permute-done | bytes 8224 | tf_op jit(solution)/shard_map/ppermute | solution.py:388
  45.4 9.3 %collective-permute-start.11 = (f32[2,16,128]{2,1,0:T(8,128)S(1)}, f32[2,16,128]{2,1,0:T(8,128)S(1)}, u32[]{:S(2)}, u32[]{:S(2)}) collective-permute-start(f32[2,16,128]{2,1,0:T(8,128)S(1)} %pad_maximum_fusion.1), channel_id=1, source_target_pairs={{4,8},{8,4},{12,16},{16,12},{20,24},{24,20},{28,32},{32,28},{36,40... | collective-permute-start | bytes 49160 | tf_op jit(solution)/shard_map/ppermute | solution.py:388
  54.7 0.1 collective-permute-start.10
  54.8 2.5 %shard_map.96 = (f32[2,16,16,128]{3,2,1,0:T(8,128)}, f32[6,2,16,16,128]{4,3,2,1,0:T(8,128)}, f32[2,16,16,128]{3,2,1,0:T(8,128)S(1)}, f32[4,2,16,16,128]{4,3,2,1,0:T(8,128)S(1)}, f32[3,2,16,16,128]{4,3,2,1,0:T(8,128)S(1)}) custom-call(f32[2,16,16,128]{3,2,1,0:T(8,128)S(1)} %get-tuple-element.34.val, f32[2,16,16,128]{3,2,1,0:T(8,128)S(1)} %get-tuple-element.43.u1, ...), custom_call_target="tpu_custom_call" | custom-call | flops 7864320 | bytes 4194304 | tf_op jit(solution)/shard_map/pallas_call | solution.py:372
  57.3 1.2 %collective-permute-done.10.ca = f32[2,16,128]{2,1,0:T(8,128)S(1)} collective-permute-done((f32[2,16,128]{2,1,0:T(8,128)S(1)}, f32[2,16,128]{2,1,0:T(8,128)S(1)}, u32[]{:S(2)}, u32[]{:S(2)}) %collective-permute-start.10) | collective-permute-done | bytes 16416 | tf_op jit(solution)/shard_map/ppermute | solution.py:388
  58.5 1.6 %shard_map.97 = (f32[2,16,16,128]{3,2,1,0:T(8,128)}, f32[4,2,16,16,128]{4,3,2,1,0:T(8,128)}, f32[6,2,16,16,128]{4,3,2,1,0:T(8,128)}) custom-call(f32[4,2,16,16,128]{4,3,2,1,0:T(8,128)S(1)} %copy-done.1, f32[6,2,16,16,128]{4,3,2,1,0:T(8,128)S(1)} %copy-done, f32[2,16,16,128]{3,2,1,0:T(8,128)S(1)} %get-tuple-element.32.inv, ...), custom_call_target="tpu_custom_call", output_to_operand_aliasing={{2}: (11, {})} | custom-call | flops 2621440 | bytes 4194304 | tf_op jit(solution)/shard_map/pallas_call | solution.py:372
  (13 shorter events, 0.0 us)
Async XLA Ops:
  0.6 25.3 %copy-start = (f32[6,2,16,16,128]{4,3,2,1,0:T(8,128)S(1)}, f32[6,2,16,16,128]{4,3,2,1,0:T(8,128)}, u32[]{:S(2)}) copy-start(f32[6,2,16,16,128]{4,3,2,1,0:T(8,128)} %crs.7) | copy-start | bytes 4718596
  0.6 25.3 %copy-start.1 = (f32[4,2,16,16,128]{4,3,2,1,0:T(8,128)S(1)}, f32[4,2,16,16,128]{4,3,2,1,0:T(8,128)}, u32[]{:S(2)}) copy-start(f32[4,2,16,16,128]{4,3,2,1,0:T(8,128)} %dif.7) | copy-start | bytes 3145732
  3.7 31.0 %collective-permute-start.2 = (f32[2,16,16,128]{3,2,1,0:T(8,128)S(1)}, f32[2,16,16,128]{3,2,1,0:T(8,128)S(1)}, u32[]{:S(2)}, u32[]{:S(2)}) collective-permute-start(f32[2,16,16,128]{3,2,1,0:T(8,128)S(1)} %get-tuple-element.41), channel_id=1, source_target_pairs={{0,4},{4,0},{8,12},{12,8},{16,20},{20,16},{24,28},{28,24},{32,36},... | collective-permute-start | bytes 786440 | tf_op jit(solution)/shard_map/ppermute | solution.py:388
  5.3 29.4 %collective-permute-start.3 = (f32[2,16,16,128]{3,2,1,0:T(8,128)S(1)}, f32[2,16,16,128]{3,2,1,0:T(8,128)S(1)}, u32[]{:S(2)}, u32[]{:S(2)}) collective-permute-start(f32[2,16,16,128]{3,2,1,0:T(8,128)S(1)} %get-tuple-element.42), channel_id=1, source_target_pairs={{4,8},{8,4},{12,16},{16,12},{20,24},{24,20},{28,32},{32,28},{36,40... | collective-permute-start | bytes 786440 | tf_op jit(solution)/shard_map/ppermute | solution.py:388
  14.3 3.1 %collective-permute-start = (f32[16,128]{1,0:T(8,128)S(1)}, f32[16,128]{1,0:T(8,128)S(1)}, u32[]{:S(2)}, u32[]{:S(2)}) collective-permute-start(f32[16,128]{1,0:T(8,128)S(1)} %get-tuple-element.37), channel_id=1, source_target_pairs={{0,1},{1,0},{2,3},{3,2},{4,5},{5,4},{6,7},{7,6},{8,9},{9,8},{10,11... | collective-permute-start | bytes 24584 | tf_op jit(solution)/shard_map/ppermute | solution.py:388
  14.4 9.5 %collective-permute-start.1 = (f32[16,128]{1,0:T(8,128)S(1)}, f32[16,128]{1,0:T(8,128)S(1)}, u32[]{:S(2)}, u32[]{:S(2)}) collective-permute-start(f32[16,128]{1,0:T(8,128)S(1)} %get-tuple-element.38), channel_id=1, source_target_pairs={{1,2},{2,1},{5,6},{6,5},{9,10},{10,9},{13,14},{14,13},{17,18},{18,... | collective-permute-start | bytes 24584 | tf_op jit(solution)/shard_map/ppermute | solution.py:388
  23.9 10.7 %collective-permute-start.5 = (f32[2,16,128]{2,1,0:T(8,128)S(1)}, f32[2,16,128]{2,1,0:T(8,128)S(1)}, u32[]{:S(2)}, u32[]{:S(2)}) collective-permute-start(f32[2,16,128]{2,1,0:T(8,128)S(1)} %pad_maximum_fusion), channel_id=1, source_target_pairs={{4,8},{8,4},{12,16},{16,12},{20,24},{24,20},{28,32},{32,28},{36,40... | collective-permute-start | bytes 49160 | tf_op jit(solution)/shard_map/ppermute | solution.py:388
  25.9 8.8 %collective-permute-start.4 = (f32[2,16,128]{2,1,0:T(8,128)S(1)}, f32[2,16,128]{2,1,0:T(8,128)S(1)}, u32[]{:S(2)}, u32[]{:S(2)}) collective-permute-start(f32[2,16,128]{2,1,0:T(8,128)S(1)} %pad_maximum_fusion), channel_id=1, source_target_pairs={{0,4},{4,0},{8,12},{12,8},{16,20},{20,16},{24,28},{28,24},{32,36},... | collective-permute-start | bytes 49160 | tf_op jit(solution)/shard_map/ppermute | solution.py:388
  26.0 8.7 %copy-start.2 = (f32[2,16,16,128]{3,2,1,0:T(8,128)S(1)}, f32[2,16,16,128]{3,2,1,0:T(8,128)}, u32[]{:S(2)}) copy-start(f32[2,16,16,128]{3,2,1,0:T(8,128)} %pay.1) | copy-start | bytes 786436
  36.0 22.5 %collective-permute-start.8 = (f32[2,16,16,128]{3,2,1,0:T(8,128)S(1)}, f32[2,16,16,128]{3,2,1,0:T(8,128)S(1)}, u32[]{:S(2)}, u32[]{:S(2)}) collective-permute-start(f32[2,16,16,128]{3,2,1,0:T(8,128)S(1)} %get-tuple-element.53), channel_id=1, source_target_pairs={{0,4},{4,0},{8,12},{12,8},{16,20},{20,16},{24,28},{28,24},{32,36},... | collective-permute-start | bytes 786440 | tf_op jit(solution)/shard_map/ppermute | solution.py:388
  36.1 22.4 %collective-permute-start.9 = (f32[2,16,16,128]{3,2,1,0:T(8,128)S(1)}, f32[2,16,16,128]{3,2,1,0:T(8,128)S(1)}, u32[]{:S(2)}, u32[]{:S(2)}) collective-permute-start(f32[2,16,16,128]{3,2,1,0:T(8,128)S(1)} %get-tuple-element.54), channel_id=1, source_target_pairs={{4,8},{8,4},{12,16},{16,12},{20,24},{24,20},{28,32},{32,28},{36,40... | collective-permute-start | bytes 786440 | tf_op jit(solution)/shard_map/ppermute | solution.py:388
  40.3 2.0 %collective-permute-start.6 = (f32[16,128]{1,0:T(8,128)S(1)}, f32[16,128]{1,0:T(8,128)S(1)}, u32[]{:S(2)}, u32[]{:S(2)}) collective-permute-start(f32[16,128]{1,0:T(8,128)S(1)} %get-tuple-element.48), channel_id=1, source_target_pairs={{0,1},{1,0},{2,3},{3,2},{4,5},{5,4},{6,7},{7,6},{8,9},{9,8},{10,11... | collective-permute-start | bytes 24584 | tf_op jit(solution)/shard_map/ppermute | solution.py:388
  40.4 5.0 %collective-permute-start.7 = (f32[16,128]{1,0:T(8,128)S(1)}, f32[16,128]{1,0:T(8,128)S(1)}, u32[]{:S(2)}, u32[]{:S(2)}) collective-permute-start(f32[16,128]{1,0:T(8,128)S(1)} %get-tuple-element.49), channel_id=1, source_target_pairs={{1,2},{2,1},{5,6},{6,5},{9,10},{10,9},{13,14},{14,13},{17,18},{18,... | collective-permute-start | bytes 24584 | tf_op jit(solution)/shard_map/ppermute | solution.py:388
  45.4 11.9 %collective-permute-start.11 = (f32[2,16,128]{2,1,0:T(8,128)S(1)}, f32[2,16,128]{2,1,0:T(8,128)S(1)}, u32[]{:S(2)}, u32[]{:S(2)}) collective-permute-start(f32[2,16,128]{2,1,0:T(8,128)S(1)} %pad_maximum_fusion.1), channel_id=1, source_target_pairs={{4,8},{8,4},{12,16},{16,12},{20,24},{24,20},{28,32},{32,28},{36,40... | collective-permute-start | bytes 49160 | tf_op jit(solution)/shard_map/ppermute | solution.py:388
  54.7 3.8 %collective-permute-start.10 = (f32[2,16,128]{2,1,0:T(8,128)S(1)}, f32[2,16,128]{2,1,0:T(8,128)S(1)}, u32[]{:S(2)}, u32[]{:S(2)}) collective-permute-start(f32[2,16,128]{2,1,0:T(8,128)S(1)} %pad_maximum_fusion.1), channel_id=1, source_target_pairs={{0,4},{4,0},{8,12},{12,8},{16,20},{20,16},{24,28},{28,24},{32,36},... | collective-permute-start | bytes 49160 | tf_op jit(solution)/shard_map/ppermute | solution.py:388

commit v3 on v2

--- a/solution.py
+++ b/solution.py
@@ -1,3 +1,5 @@
+import functools
+
 import jax
 import jax.numpy as jnp
 from jax import lax
@@ -8,8 +10,8 @@
 F32 = jnp.float32
 TILE = (16, 128)
 BLOCK = (2, 16, 16, 128)
-CHUNK = 4
-CHUNKS = 16 // CHUNK
+OUT_CHUNK = 8
+IN_CHUNK = 8
 
 
 def lanes():
@@ -223,8 +225,8 @@
 
 def kernel_a(cot_h, flg_h, dif_h, crs_h, val_h, msg_a, msg_b, n1, n2, inv, w2, adj, cot, flg, val, dif, crs, sems, *scratch):
     copies = []
-    for c in range(CHUNKS):
-        span = pl.ds(c * CHUNK, CHUNK)
+    for c in range(16 // IN_CHUNK):
+        span = pl.ds(c * IN_CHUNK, IN_CHUNK)
         group = []
         for k, (src, dst) in enumerate(((cot_h, cot), (flg_h, flg), (val_h, val))):
             group.append(pltpu.make_async_copy(src.at[:, span], dst.at[:, span], sems.at[c, k]))
@@ -235,8 +237,8 @@
         copies.append(group)
 
     def weight(r, i):
-        if r == 0 and i % CHUNK == 0:
-            for copy in copies[i // CHUNK]:
+        if r == 0 and i % IN_CHUNK == 0:
+            for copy in copies[i // IN_CHUNK]:
                 copy.wait()
         recip = 1.0 / (1.0 + 2.0 * (dif[0, r, i] + dif[1, r, i] + dif[2, r, i] + dif[3, r, i]))
         inv[r, i] = recip
@@ -330,32 +332,42 @@
         copy.wait()
 
 
-def kernel_c(dif, crs, inv, w2, part, pd, pc, ra, rb, ca, cb, gc_in, gval, gd, gc, out_val, out_d, out_c, sems):
-    del gc_in
-    beyond = outer(ra, rb, ca, cb)
-    column = corner_overhang(ca, cb)
+def kernel_c(side, dif, crs, inv, w2, part, pd, pc, msg, cor, *rest):
+    gval, gd, gc, out_val, out_d, out_c, sems = rest[-7:]
+    row, lane = rows(), lanes()
+    odd = wide_odd()
+    r = 1 - odd if side == 0 else odd
+    high = r == 1
+    sign = 0.25 * (2 * r - 1).astype(F32)
+    packs = narrow_sides(cor[0], cor[1])
+    right, left = (jnp.where(high, pack, lane_roll(pack, -16)) for pack in packs)
+    column = columns(*(jnp.where(high, lane_roll(pack, -32), lane_roll(pack, -80)) for pack in packs))
     copies = []
     for i in range(16):
-        for r in range(2):
-            x, more = beyond(r, i)
-            value = dif[0, r, i] * x
-            for k in range(3):
-                value = value + crs[k, r, i] * more[k]
-            v = w2[r, i]
-            change = (2.0 * inv[r, i]) * v * value
-            out_d[0, r, i] = pd[0, r, i] + (v * x - change)
-            for k in range(1, 4):
-                out_d[k, r, i] = pd[k, r, i] - change
-            for k in range(3):
-                out_c[k, r, i] = pc[k, r, i] + v * more[k]
-            out_val[r, i] = part[r, i] + from_wide(ra, rb, 1, r, i) + column(r, i)
-        if i % CHUNK == CHUNK - 1:
-            c = i // CHUNK
-            span = pl.ds(c * CHUNK, CHUNK)
+        x = msg[0, i]
+        d1 = both(msg, 0, i)[1]
+        d2 = up2(x, row) - down2(x, row)
+        plus = jnp.where(lane == 127, lane_roll(right, 127 - i), lane_roll(x, 127))
+        minus = jnp.where(lane == 0, lane_roll(left, -i), lane_roll(x, 1))
+        more = (sign * d1, sign * d2, sign * (plus - minus))
+        value = dif[0, r, i] * x
+        for k in range(3):
+            value = value + crs[k, r, i] * more[k]
+        v = w2[r, i]
+        change = (2.0 * inv[r, i]) * v * value
+        out_d[0, i] = pd[0, r, i] + (v * x - change)
+        for k in range(1, 4):
+            out_d[k, i] = pd[k, r, i] - change
+        for k in range(3):
+            out_c[k, i] = pc[k, r, i] + v * more[k]
+        out_val[i] = part[r, i] + msg[1, i] + column(0, i)
+        if i % OUT_CHUNK == OUT_CHUNK - 1:
+            c = i // OUT_CHUNK
+            span = pl.ds(c * OUT_CHUNK, OUT_CHUNK)
             group = [
-                pltpu.make_async_copy(out_d.at[:, :, span], gd.at[:, :, span], sems.at[c, 0]),
-                pltpu.make_async_copy(out_c.at[:, :, span], gc.at[pl.ds(0, 3), :, span], sems.at[c, 1]),
-                pltpu.make_async_copy(out_val.at[:, span], gval.at[:, span], sems.at[c, 2]),
+                pltpu.make_async_copy(out_d.at[:, span], gd.at[:, r, span], sems.at[c, 0]),
+                pltpu.make_async_copy(out_c.at[:, span], gc.at[pl.ds(0, 3), r, span], sems.at[c, 1]),
+                pltpu.make_async_copy(out_val.at[span], gval.at[r, span], sems.at[c, 2]),
             ]
             for copy in group:
                 copy.start()
@@ -407,7 +419,7 @@
     msg_a, msg_b, n1, n2, inv, w2, adj, cot, flg, val = call(
         kernel_a,
         [*sends, block, block, block, block, (BLOCK, V, jnp.int32), block],
-        [pltpu.VMEM(four, F32), pltpu.VMEM(six, F32), pltpu.SemaphoreType.DMA((CHUNKS, 5)), *ADJOINT_SCRATCH],
+        [pltpu.VMEM(four, F32), pltpu.VMEM(six, F32), pltpu.SemaphoreType.DMA((16 // IN_CHUNK, 5)), *ADJOINT_SCRATCH],
         40 << 16,
         (cotangent, flags[0], diffusion, cross_terms, value_in),
         [H] * 5,
@@ -430,14 +442,13 @@
         120 << 16,
         (val, u1, flg, diffusion, cross_terms, inv, total, w1, w2, cot, adj1, adj0, ra, rb, r1, r2, ca, cb, s1, s2),
     )
+    half = (16, *TILE)
+    scratch = [pltpu.VMEM(half, F32), pltpu.VMEM((4, *half), F32), pltpu.VMEM((3, *half), F32), pltpu.SemaphoreType.DMA((16 // OUT_CHUNK, 3))]
+    outs = [(BLOCK, H), (four, H), (six, H)]
+    given = (diffusion, cross_terms, inv, w2, part, pd, pc)
+    gval, gd, gc = call(functools.partial(kernel_c, 0), outs, scratch, 20 << 16, (*given, sa, da, gc), [V] * 9 + [H], {9: 2})
     gval, gd, gc = call(
-        kernel_c,
-        [(BLOCK, H), (four, H), (six, H)],
-        [pltpu.VMEM(BLOCK, F32), pltpu.VMEM(four, F32), pltpu.VMEM((3, *BLOCK), F32), pltpu.SemaphoreType.DMA((CHUNKS, 3))],
-        40 << 16,
-        (diffusion, cross_terms, inv, w2, part, pd, pc, sa, sb, da, db, gc),
-        [V] * 11 + [H],
-        {11: 2},
+        functools.partial(kernel_c, 1), outs, scratch, 20 << 16, (*given, sb, db, gval, gd, gc), [V] * 9 + [H] * 3, {9: 0, 10: 1, 11: 2}
     )
     return gval, gpay, gd, gc
 

time: 60.4 us -> 59.9 us (level)
  waiting for transfers between devices: 18.8 us -> 17.6 us
  Pallas kernels: 9.03 us -> 9.88 us
    ppermute x12, waiting for transfers between devices: 18.8 us -> 17.6 us  [swap(): return lax.ppermute(x, axis, pairs)]
    pallas_call x5 -> x6, Pallas kernels: 9.03 us -> 9.88 us  [call(): pl.pallas_call(kernel, out_shape=[jax.ShapeDtypeStruct(out[0], out[2] if...]
  transfers between devices with their start and end apart: 12 -> 12, of which waited for: 4 -> 3; matrix products, arithmetic and copies ran while one was open for 0% -> 0% of each run, Pallas kernels for 5% -> 7%
where the time goes in v3:
time: 59.9 us; the launch traced here: 59.7 us
  starting transfers between devices  31.3 us (52%)
  waiting for transfers between devices  17.6 us (29%)
  Pallas kernels  9.88 us (16%)
  between operations  0.85 us (1%)
    ppermute x12, starting transfers between devices, swap(): return lax.ppermute(x, axis, pairs)  31.3 us
    ppermute x12, waiting for transfers between devices, swap(): return lax.ppermute(x, axis, pairs)  17.6 us
    pallas_call x6, Pallas kernels, call(): pl.pallas_call(kernel, out_shape=[jax.ShapeDtypeStruct(out[0], out[2] if...  9.88 us
  transfers between devices with their start and end apart: 12, of which 3 were waited for; matrix products, arithmetic and copies ran while one was open for 0% of the time, Pallas kernels for 7%

profile of v3, /device:TPU:56, one launch (start us, length us, event | category | flops | bytes accessed | tf_op | source)
XLA Modules:
  0.0 59.7 jit_solution(535191354534447928)
XLA Ops:
  0.7 3.0 %shard_map.93 = (f32[2,16,16,128]{3,2,1,0:T(8,128)S(1)}, f32[2,16,16,128]{3,2,1,0:T(8,128)S(1)}, f32[16,128]{1,0:T(8,128)S(1)}, f32[16,128]{1,0:T(8,128)S(1)}, f...) custom-call(f32[2,16,16,128]{3,2,1,0:T(8,128)} %cot_h.1, ...), custom_call_target="tpu_custom_call" | custom-call | flops 2621440 | bytes 4194304 | tf_op jit(solution)/shard_map/pallas_call | solution.py:384
  3.7 1.6 %collective-permute-start.2 = (f32[2,16,16,128]{3,2,1,0:T(8,128)S(1)}, f32[2,16,16,128]{3,2,1,0:T(8,128)S(1)}, u32[]{:S(2)}, u32[]{:S(2)}) collective-permute-start(f32[2,16,16,128]{3,2,1,0:T(8,128)S(1)} %get-tuple-element.44), channel_id=1, source_target_pairs={{0,4},{4,0},{8,12},{12,8},{16,20},{20,16},{24,28},{28,24},{32,36},... | collective-permute-start | bytes 786440 | tf_op jit(solution)/shard_map/ppermute | solution.py:400
  5.3 9.0 %collective-permute-start.3 = (f32[2,16,16,128]{3,2,1,0:T(8,128)S(1)}, f32[2,16,16,128]{3,2,1,0:T(8,128)S(1)}, u32[]{:S(2)}, u32[]{:S(2)}) collective-permute-start(f32[2,16,16,128]{3,2,1,0:T(8,128)S(1)} %get-tuple-element.45), channel_id=1, source_target_pairs={{4,8},{8,4},{12,16},{16,12},{20,24},{24,20},{28,32},{32,28},{36,40... | collective-permute-start | bytes 786440 | tf_op jit(solution)/shard_map/ppermute | solution.py:400
  14.3 0.1 collective-permute-start
  14.4 3.0 %collective-permute-start.1 = (f32[16,128]{1,0:T(8,128)S(1)}, f32[16,128]{1,0:T(8,128)S(1)}, u32[]{:S(2)}, u32[]{:S(2)}) collective-permute-start(f32[16,128]{1,0:T(8,128)S(1)} %get-tuple-element.41), channel_id=1, source_target_pairs={{1,2},{2,1},{5,6},{6,5},{9,10},{10,9},{13,14},{14,13},{17,18},{18,... | collective-permute-start | bytes 24584 | tf_op jit(solution)/shard_map/ppermute | solution.py:400
  17.4 0.0 collective-permute-done.r1
  17.4 6.5 %collective-permute-done.1.r2 = f32[16,128]{1,0:T(8,128)S(1)} collective-permute-done((f32[16,128]{1,0:T(8,128)S(1)}, f32[16,128]{1,0:T(8,128)S(1)}, u32[]{:S(2)}, u32[]{:S(2)}) %collective-permute-start.1) | collective-permute-done | bytes 8224 | tf_op jit(solution)/shard_map/ppermute | solution.py:400
  23.9 1.9 %collective-permute-start.5 = (f32[2,16,128]{2,1,0:T(8,128)S(1)}, f32[2,16,128]{2,1,0:T(8,128)S(1)}, u32[]{:S(2)}, u32[]{:S(2)}) collective-permute-start(f32[2,16,128]{2,1,0:T(8,128)S(1)} %pad_maximum_fusion), channel_id=1, source_target_pairs={{4,8},{8,4},{12,16},{16,12},{20,24},{24,20},{28,32},{32,28},{36,40... | collective-permute-start | bytes 49160 | tf_op jit(solution)/shard_map/ppermute | solution.py:400
  25.8 0.1 collective-permute-start.4
  25.9 0.0 copy-start.2
  26.0 0.6 %shard_map.94 = (f32[2,16,16,128]{3,2,1,0:T(8,128)S(1)}, f32[2,16,16,128]{3,2,1,0:T(8,128)S(1)}) custom-call(f32[2,16,16,128]{3,2,1,0:T(8,128)S(1)} %get-tuple-element.37.val, f32[4,2,16,16,128]{4,3,2,1,0:T(8,128)S(1)} %copy-done.1, f32[6,2,16,16,128]{4,3,2,1,0:T(8,128)S(1)} %copy-done, f32[2,16,16,128]{3,2,1,0:T(8,128)S(1)} %get-tuple-element.39.adj_in, ...), custom_call_target="tpu_custom_call" | custom-call | flops 2621440 | bytes 4194304 | tf_op jit(solution)/shard_map/pallas_call | solution.py:384
  26.6 8.1 %collective-permute-done.5.cb = f32[2,16,128]{2,1,0:T(8,128)S(1)} collective-permute-done((f32[2,16,128]{2,1,0:T(8,128)S(1)}, f32[2,16,128]{2,1,0:T(8,128)S(1)}, u32[]{:S(2)}, u32[]{:S(2)}) %collective-permute-start.5) | collective-permute-done | bytes 16416 | tf_op jit(solution)/shard_map/ppermute | solution.py:400
  34.6 0.0 collective-permute-done.4.ca
  34.6 0.0 collective-permute-done.2.ra
  34.7 1.3 %shard_map.95 = (f32[2,16,16,128]{3,2,1,0:T(8,128)S(1)}, f32[2,16,16,128]{3,2,1,0:T(8,128)S(1)}, f32[16,128]{1,0:T(8,128)S(1)}, f32[16,128]{1,0:T(8,128)S(1)}, f...) custom-call(f32[2,16,16,128]{3,2,1,0:T(8,128)S(1)} %copy-done.2, ...), custom_call_target="tpu_custom_call" | custom-call | flops 3932160 | bytes 4194304 | tf_op jit(solution)/shard_map/pallas_call | solution.py:384
  35.9 0.1 collective-permute-start.10
  36.0 4.2 %collective-permute-start.8 = (f32[2,16,16,128]{3,2,1,0:T(8,128)S(1)}, f32[2,16,16,128]{3,2,1,0:T(8,128)S(1)}, u32[]{:S(2)}, u32[]{:S(2)}) collective-permute-start(f32[2,16,16,128]{3,2,1,0:T(8,128)S(1)} %get-tuple-element.56), channel_id=1, source_target_pairs={{4,8},{8,4},{12,16},{16,12},{20,24},{24,20},{28,32},{32,28},{36,40... | collective-permute-start | bytes 786440 | tf_op jit(solution)/shard_map/ppermute | solution.py:400
  40.2 0.1 collective-permute-start.6
  40.3 1.9 %collective-permute-start.7 = (f32[16,128]{1,0:T(8,128)S(1)}, f32[16,128]{1,0:T(8,128)S(1)}, u32[]{:S(2)}, u32[]{:S(2)}) collective-permute-start(f32[16,128]{1,0:T(8,128)S(1)} %get-tuple-element.52), channel_id=1, source_target_pairs={{1,2},{2,1},{5,6},{6,5},{9,10},{10,9},{13,14},{14,13},{17,18},{18,... | collective-permute-start | bytes 24584 | tf_op jit(solution)/shard_map/ppermute | solution.py:400
  42.3 3.0 %collective-permute-done.7.s2 = f32[16,128]{1,0:T(8,128)S(1)} collective-permute-done((f32[16,128]{1,0:T(8,128)S(1)}, f32[16,128]{1,0:T(8,128)S(1)}, u32[]{:S(2)}, u32[]{:S(2)}) %collective-permute-start.7) | collective-permute-done | bytes 8224 | tf_op jit(solution)/shard_map/ppermute | solution.py:400
  45.3 9.3 %collective-permute-start.9 = (f32[2,16,128]{2,1,0:T(8,128)S(1)}, f32[2,16,128]{2,1,0:T(8,128)S(1)}, u32[]{:S(2)}, u32[]{:S(2)}) collective-permute-start(f32[2,16,128]{2,1,0:T(8,128)S(1)} %pad_maximum_fusion.1), channel_id=1, source_target_pairs={{4,8},{8,4},{12,16},{16,12},{20,24},{24,20},{28,32},{32,28},{36,40... | collective-permute-start | bytes 49160 | tf_op jit(solution)/shard_map/ppermute | solution.py:400
  54.6 2.5 %shard_map.96 = (f32[2,16,16,128]{3,2,1,0:T(8,128)}, f32[6,2,16,16,128]{4,3,2,1,0:T(8,128)}, f32[2,16,16,128]{3,2,1,0:T(8,128)S(1)}, f32[4,2,16,16,128]{4,3,2,1,0:T(8,128)S(1)}, f32[3,2,16,16,128]{4,3,2,1,0:T(8,128)S(1)}) custom-call(f32[2,16,16,128]{3,2,1,0:T(8,128)S(1)} %get-tuple-element.37.val, f32[2,16,16,128]{3,2,1,0:T(8,128)S(1)} %get-tuple-element.46.u1, ...), custom_call_target="tpu_custom_call" | custom-call | flops 7864320 | bytes 4194304 | tf_op jit(solution)/shard_map/pallas_call | solution.py:384
  57.2 1.2 %shard_map.97 = (f32[2,16,16,128]{3,2,1,0:T(8,128)}, f32[4,2,16,16,128]{4,3,2,1,0:T(8,128)}, f32[6,2,16,16,128]{4,3,2,1,0:T(8,128)}) custom-call(f32[4,2,16,16,128]{4,3,2,1,0:T(8,128)S(1)} %copy-done.1, f32[6,2,16,16,128]{4,3,2,1,0:T(8,128)S(1)} %copy-done, f32[2,16,16,128]{3,2,1,0:T(8,128)S(1)} %get-tuple-element.35.inv, ...), custom_call_target="tpu_custom_call", output_to_operand_aliasing={{2}: (9, {})} | custom-call | flops 1310720 | bytes 4194304 | tf_op jit(solution)/shard_map/pallas_call | solution.py:384
  58.4 1.2 %shard_map.98 = (f32[2,16,16,128]{3,2,1,0:T(8,128)}, f32[4,2,16,16,128]{4,3,2,1,0:T(8,128)}, f32[6,2,16,16,128]{4,3,2,1,0:T(8,128)}) custom-call(f32[4,2,16,16,128]{4,3,2,1,0:T(8,128)S(1)} %copy-done.1, f32[6,2,16,16,128]{4,3,2,1,0:T(8,128)S(1)} %copy-done, ...), custom_call_target="tpu_custom_call", output_to_operand_aliasing={{0}: (9, {}), {1}: (10, {}), {2}: (11, {})} | custom-call | flops 1310720 | bytes 4194304 | tf_op jit(solution)/shard_map/pallas_call | solution.py:384
  (14 shorter events, 0.0 us)
Async XLA Ops:
  0.6 25.3 %copy-start = (f32[6,2,16,16,128]{4,3,2,1,0:T(8,128)S(1)}, f32[6,2,16,16,128]{4,3,2,1,0:T(8,128)}, u32[]{:S(2)}) copy-start(f32[6,2,16,16,128]{4,3,2,1,0:T(8,128)} %crs.9) | copy-start | bytes 4718596
  0.6 25.3 %copy-start.1 = (f32[4,2,16,16,128]{4,3,2,1,0:T(8,128)S(1)}, f32[4,2,16,16,128]{4,3,2,1,0:T(8,128)}, u32[]{:S(2)}) copy-start(f32[4,2,16,16,128]{4,3,2,1,0:T(8,128)} %dif.9) | copy-start | bytes 3145732
  3.7 31.0 %collective-permute-start.2 = (f32[2,16,16,128]{3,2,1,0:T(8,128)S(1)}, f32[2,16,16,128]{3,2,1,0:T(8,128)S(1)}, u32[]{:S(2)}, u32[]{:S(2)}) collective-permute-start(f32[2,16,16,128]{3,2,1,0:T(8,128)S(1)} %get-tuple-element.44), channel_id=1, source_target_pairs={{0,4},{4,0},{8,12},{12,8},{16,20},{20,16},{24,28},{28,24},{32,36},... | collective-permute-start | bytes 786440 | tf_op jit(solution)/shard_map/ppermute | solution.py:400
  5.3 29.4 %collective-permute-start.3 = (f32[2,16,16,128]{3,2,1,0:T(8,128)S(1)}, f32[2,16,16,128]{3,2,1,0:T(8,128)S(1)}, u32[]{:S(2)}, u32[]{:S(2)}) collective-permute-start(f32[2,16,16,128]{3,2,1,0:T(8,128)S(1)} %get-tuple-element.45), channel_id=1, source_target_pairs={{4,8},{8,4},{12,16},{16,12},{20,24},{24,20},{28,32},{32,28},{36,40... | collective-permute-start | bytes 786440 | tf_op jit(solution)/shard_map/ppermute | solution.py:400
  14.3 3.1 %collective-permute-start = (f32[16,128]{1,0:T(8,128)S(1)}, f32[16,128]{1,0:T(8,128)S(1)}, u32[]{:S(2)}, u32[]{:S(2)}) collective-permute-start(f32[16,128]{1,0:T(8,128)S(1)} %get-tuple-element.40), channel_id=1, source_target_pairs={{0,1},{1,0},{2,3},{3,2},{4,5},{5,4},{6,7},{7,6},{8,9},{9,8},{10,11... | collective-permute-start | bytes 24584 | tf_op jit(solution)/shard_map/ppermute | solution.py:400
  14.4 9.5 %collective-permute-start.1 = (f32[16,128]{1,0:T(8,128)S(1)}, f32[16,128]{1,0:T(8,128)S(1)}, u32[]{:S(2)}, u32[]{:S(2)}) collective-permute-start(f32[16,128]{1,0:T(8,128)S(1)} %get-tuple-element.41), channel_id=1, source_target_pairs={{1,2},{2,1},{5,6},{6,5},{9,10},{10,9},{13,14},{14,13},{17,18},{18,... | collective-permute-start | bytes 24584 | tf_op jit(solution)/shard_map/ppermute | solution.py:400
  23.9 10.7 %collective-permute-start.5 = (f32[2,16,128]{2,1,0:T(8,128)S(1)}, f32[2,16,128]{2,1,0:T(8,128)S(1)}, u32[]{:S(2)}, u32[]{:S(2)}) collective-permute-start(f32[2,16,128]{2,1,0:T(8,128)S(1)} %pad_maximum_fusion), channel_id=1, source_target_pairs={{4,8},{8,4},{12,16},{16,12},{20,24},{24,20},{28,32},{32,28},{36,40... | collective-permute-start | bytes 49160 | tf_op jit(solution)/shard_map/ppermute | solution.py:400
  25.8 8.8 %collective-permute-start.4 = (f32[2,16,128]{2,1,0:T(8,128)S(1)}, f32[2,16,128]{2,1,0:T(8,128)S(1)}, u32[]{:S(2)}, u32[]{:S(2)}) collective-permute-start(f32[2,16,128]{2,1,0:T(8,128)S(1)} %pad_maximum_fusion), channel_id=1, source_target_pairs={{0,4},{4,0},{8,12},{12,8},{16,20},{20,16},{24,28},{28,24},{32,36},... | collective-permute-start | bytes 49160 | tf_op jit(solution)/shard_map/ppermute | solution.py:400
  25.9 8.7 %copy-start.2 = (f32[2,16,16,128]{3,2,1,0:T(8,128)S(1)}, f32[2,16,16,128]{3,2,1,0:T(8,128)}, u32[]{:S(2)}) copy-start(f32[2,16,16,128]{3,2,1,0:T(8,128)} %pay.1) | copy-start | bytes 786436
  35.9 21.2 %collective-permute-start.10 = (f32[2,16,16,128]{3,2,1,0:T(8,128)S(1)}, f32[2,16,16,128]{3,2,1,0:T(8,128)S(1)}, u32[]{:S(2)}, u32[]{:S(2)}) collective-permute-start(f32[2,16,16,128]{3,2,1,0:T(8,128)S(1)} %get-tuple-element.57), channel_id=1, source_target_pairs={{0,4},{4,0},{8,12},{12,8},{16,20},{20,16},{24,28},{28,24},{32,36},... | collective-permute-start | bytes 786440 | tf_op jit(solution)/shard_map/ppermute | solution.py:400
  36.0 22.4 %collective-permute-start.8 = (f32[2,16,16,128]{3,2,1,0:T(8,128)S(1)}, f32[2,16,16,128]{3,2,1,0:T(8,128)S(1)}, u32[]{:S(2)}, u32[]{:S(2)}) collective-permute-start(f32[2,16,16,128]{3,2,1,0:T(8,128)S(1)} %get-tuple-element.56), channel_id=1, source_target_pairs={{4,8},{8,4},{12,16},{16,12},{20,24},{24,20},{28,32},{32,28},{36,40... | collective-permute-start | bytes 786440 | tf_op jit(solution)/shard_map/ppermute | solution.py:400
  40.2 2.0 %collective-permute-start.6 = (f32[16,128]{1,0:T(8,128)S(1)}, f32[16,128]{1,0:T(8,128)S(1)}, u32[]{:S(2)}, u32[]{:S(2)}) collective-permute-start(f32[16,128]{1,0:T(8,128)S(1)} %get-tuple-element.51), channel_id=1, source_target_pairs={{0,1},{1,0},{2,3},{3,2},{4,5},{5,4},{6,7},{7,6},{8,9},{9,8},{10,11... | collective-permute-start | bytes 24584 | tf_op jit(solution)/shard_map/ppermute | solution.py:400
  40.3 5.0 %collective-permute-start.7 = (f32[16,128]{1,0:T(8,128)S(1)}, f32[16,128]{1,0:T(8,128)S(1)}, u32[]{:S(2)}, u32[]{:S(2)}) collective-permute-start(f32[16,128]{1,0:T(8,128)S(1)} %get-tuple-element.52), channel_id=1, source_target_pairs={{1,2},{2,1},{5,6},{6,5},{9,10},{10,9},{13,14},{14,13},{17,18},{18,... | collective-permute-start | bytes 24584 | tf_op jit(solution)/shard_map/ppermute | solution.py:400
  45.3 11.8 %collective-permute-start.11 = (f32[2,16,128]{2,1,0:T(8,128)S(1)}, f32[2,16,128]{2,1,0:T(8,128)S(1)}, u32[]{:S(2)}, u32[]{:S(2)}) collective-permute-start(f32[2,16,128]{2,1,0:T(8,128)S(1)} %pad_maximum_fusion.1), channel_id=1, source_target_pairs={{0,4},{4,0},{8,12},{12,8},{16,20},{20,16},{24,28},{28,24},{32,36},... | collective-permute-start | bytes 49160 | tf_op jit(solution)/shard_map/ppermute | solution.py:400
  45.3 13.1 %collective-permute-start.9 = (f32[2,16,128]{2,1,0:T(8,128)S(1)}, f32[2,16,128]{2,1,0:T(8,128)S(1)}, u32[]{:S(2)}, u32[]{:S(2)}) collective-permute-start(f32[2,16,128]{2,1,0:T(8,128)S(1)} %pad_maximum_fusion.1), channel_id=1, source_target_pairs={{4,8},{8,4},{12,16},{16,12},{20,24},{24,20},{28,32},{32,28},{36,40... | collective-permute-start | bytes 49160 | tf_op jit(solution)/shard_map/ppermute | solution.py:400

commit v4 on v3

--- a/solution.py
+++ b/solution.py
@@ -71,8 +71,9 @@
     return jnp.where(even, low[part, i], high[part, i])
 
 
-def adjoint(w_of, u_of, dif, crs, scratch, msg_a, msg_b, n1, n2, adj_of):
-    q1s, p01s, p12s, p13s, x2s, y2s, x3s, y3s, q0s, p02s, p03s = scratch
+def adjoint(w_of, u_of, dif, crs, parts, scratch, msg_a, msg_b, n1, n2):
+    q0s, q1s, p01s, p12s, x2s, y2s, x3s, y3s = parts
+    p13s, p02s, p03s = scratch
     row, lane = rows(), lanes()
     for i in range(16):
         w = [w_of(r, i) for r in range(2)]
@@ -111,18 +112,11 @@
             u = u_of(r, i)
             left = put(left, u, 0, r * 16 + i)
             right = put(right, u, 127, r * 16 + i)
-            f12 = both(p12s, r, i)[1]
             f13 = both(p13s, r, i)[1]
             x3 = x3s[r, i] + f13
             y3 = y3s[r, i] - f13
-            x2 = x2s[r, i] + f12
-            y2 = y2s[r, i] - f12
-            e01 = both(p01s, 1 - r, i)[1]
-            total = q0s[1 - r, i] + both(q1s, r, i)[0]
-            total = total + e01 if r == 0 else total - e01
-            total = total + up2(x2, row) + down2(y2, row)
-            total = total + jnp.where(lane == 127, 0.0, lane_roll(x3, 127)) + jnp.where(lane == 0, 0.0, lane_roll(y3, 1))
-            adj_of(r, i, total)
+            x3s[r, i] = x3
+            y3s[r, i] = y3
             left = put(left, x3, 0, 48 + r * 16 + i)
             right = put(right, y3, 127, 48 + r * 16 + i)
         p0, p1 = p03s[0, i], p03s[1, i]
@@ -142,6 +136,24 @@
     n2[...] = jnp.where(even, left, right)
 
 
+def own_adjoint(parts):
+    q0s, q1s, p01s, p12s, x2s, y2s, x3s, y3s = parts
+    row, lane = rows(), lanes()
+
+    def at(r, i):
+        f12 = both(p12s, r, i)[1]
+        x3, y3 = x3s[r, i], y3s[r, i]
+        x2 = x2s[r, i] + f12
+        y2 = y2s[r, i] - f12
+        e01 = both(p01s, 1 - r, i)[1]
+        total = q0s[1 - r, i] + both(q1s, r, i)[0]
+        total = total + e01 if r == 0 else total - e01
+        total = total + up2(x2, row) + down2(y2, row)
+        return total + jnp.where(lane == 127, 0.0, lane_roll(x3, 127)) + jnp.where(lane == 0, 0.0, lane_roll(y3, 1))
+
+    return at
+
+
 def inner(us, r1, r2, scratch):
     d2s, d3s, n2s, n3s = scratch
     row, lane = rows(), lanes()
@@ -219,11 +231,13 @@
     return columns(*merged)
 
 
-ADJOINT_SCRATCH = [pltpu.VMEM(BLOCK, F32)] * 11
+ADJOINT_SCRATCH = [pltpu.VMEM(BLOCK, F32)] * 3
+PARTS = 8
 INNER_SCRATCH = [pltpu.VMEM(BLOCK, F32)] * 4
 
 
-def kernel_a(cot_h, flg_h, dif_h, crs_h, val_h, msg_a, msg_b, n1, n2, inv, w2, adj, cot, flg, val, dif, crs, sems, *scratch):
+def kernel_a(cot_h, flg_h, dif_h, crs_h, val_h, msg_a, msg_b, n1, n2, inv, w2, cot, flg, val, *rest):
+    parts, (dif, crs, sems, *scratch) = rest[:PARTS], rest[PARTS:]
     copies = []
     for c in range(16 // IN_CHUNK):
         span = pl.ds(c * IN_CHUNK, IN_CHUNK)
@@ -246,13 +260,11 @@
         w2[r, i] = w
         return w
 
-    def keep(r, i, total):
-        adj[r, i] = total
-
-    adjoint(weight, lambda r, i: val[r, i], dif, crs, scratch, msg_a, msg_b, n1, n2, keep)
-
-
-def kernel_p(val, dif, crs, adj_in, r1, r2, total, adj, *scratch):
+    adjoint(weight, lambda r, i: val[r, i], dif, crs, parts, scratch, msg_a, msg_b, n1, n2)
+
+
+def kernel_p(val, dif, crs, r1, r2, *rest):
+    own, (total, adj, *scratch) = own_adjoint(rest[:PARTS]), rest[PARTS:]
     at = inner(val, r1, r2, scratch)
     column = narrow_overhang(r1, r2)
     for i in range(16):
@@ -264,10 +276,10 @@
             for k in range(6):
                 value = value + crs[k, r, i] * mixed[k]
             total[r, i] = value
-            adj[r, i] = adj_in[r, i] + column(r, i)
-
-
-def kernel_b(pay, flg, dif, crs, inv, total, adj_in, ra, rb, ca, cb, msg_a, msg_b, n1, n2, u1, w1, adj1, adj0, *scratch):
+            adj[r, i] = own(r, i) + column(r, i)
+
+
+def kernel_b(pay, flg, dif, crs, inv, total, adj_in, ra, rb, ca, cb, msg_a, msg_b, n1, n2, u1, w1, adj1, *rest):
     beyond = outer(ra, rb, ca, cb)
     column = corner_overhang(ca, cb)
 
@@ -285,16 +297,13 @@
         w1[r, i] = w
         return w
 
-    def keep(r, i, value):
-        adj0[r, i] = value
-
-    adjoint(weight, lambda r, i: u1[r, i], dif, crs, scratch, msg_a, msg_b, n1, n2, keep)
+    adjoint(weight, lambda r, i: u1[r, i], dif, crs, rest[:PARTS], rest[PARTS:], msg_a, msg_b, n1, n2)
 
 
 def kernel_m(
-    val, u1, flg, dif, crs, inv, total, w1, w2, cot, adj1, adj0, ra, rb, r1, r2, ca, cb, s1, s2,
-    gpay, gc, part, pd, pc, out_pay, out_gc, sems, *scratch,
+    val, u1, flg, dif, crs, inv, total, w1, w2, cot, adj1, ra, rb, r1, r2, ca, cb, s1, s2, *rest
 ):
+    own, (gpay, gc, part, pd, pc, out_pay, out_gc, sems, *scratch) = own_adjoint(rest[:PARTS]), rest[PARTS:]
     first = inner(val, r1, r2, scratch[:4])
     beyond = outer(ra, rb, ca, cb)
     second = inner(u1, s1, s2, scratch[4:])
@@ -324,7 +333,7 @@
             for k in range(3, 6):
                 out_gc[k - 3, r, i] = w * mixed[k] + v * mixed_2[k]
             out_pay[r, i] = jnp.where(flg[r, i] == 1, cot[r, i] + adj1[r, i], 0.0)
-            part[r, i] = adj0[r, i] + w + v + column(r, i)
+            part[r, i] = own(r, i) + w + v + column(r, i)
     copies = [pltpu.make_async_copy(out_pay, gpay, sems.at[0]), pltpu.make_async_copy(out_gc, gc.at[pl.ds(3, 3)], sems.at[1])]
     for copy in copies:
         copy.start()
@@ -416,20 +425,20 @@
     message = (2, 16, *TILE)
     sends = [(message, V), (message, V), (TILE, V), (TILE, V)]
     block = (BLOCK, V)
-    msg_a, msg_b, n1, n2, inv, w2, adj, cot, flg, val = call(
+    msg_a, msg_b, n1, n2, inv, w2, cot, flg, val, *parts = call(
         kernel_a,
-        [*sends, block, block, block, block, (BLOCK, V, jnp.int32), block],
+        [*sends, block, block, block, (BLOCK, V, jnp.int32), block, *[block] * PARTS],
         [pltpu.VMEM(four, F32), pltpu.VMEM(six, F32), pltpu.SemaphoreType.DMA((16 // IN_CHUNK, 5)), *ADJOINT_SCRATCH],
         40 << 16,
         (cotangent, flags[0], diffusion, cross_terms, value_in),
         [H] * 5,
-        limit=207,
+        limit=200,
     )
     ra, rb, r1, r2, ca, cb = exchange(msg_a, msg_b, n1, n2)
-    total, adj = call(kernel_p, [block, block], INNER_SCRATCH, 40 << 16, (val, diffusion, cross_terms, adj, r1, r2))
-    msg_a, msg_b, n1, n2, u1, w1, adj1, adj0 = call(
+    total, adj = call(kernel_p, [block, block], INNER_SCRATCH, 40 << 16, (val, diffusion, cross_terms, r1, r2, *parts))
+    msg_a, msg_b, n1, n2, u1, w1, adj1, *parts = call(
         kernel_b,
-        [*sends, block, block, block, block],
+        [*sends, block, block, block, *[block] * PARTS],
         ADJOINT_SCRATCH,
         60 << 16,
         (payoff, flg, diffusion, cross_terms, inv, total, adj, ra, rb, ca, cb),
@@ -440,7 +449,7 @@
         [(BLOCK, H), (six, H), block, (four, V), ((3, *BLOCK), V)],
         [pltpu.VMEM(BLOCK, F32), pltpu.VMEM((3, *BLOCK), F32), pltpu.SemaphoreType.DMA((2,)), *INNER_SCRATCH, *INNER_SCRATCH],
         120 << 16,
-        (val, u1, flg, diffusion, cross_terms, inv, total, w1, w2, cot, adj1, adj0, ra, rb, r1, r2, ca, cb, s1, s2),
+        (val, u1, flg, diffusion, cross_terms, inv, total, w1, w2, cot, adj1, ra, rb, r1, r2, ca, cb, s1, s2, *parts),
     )
     half = (16, *TILE)
     scratch = [pltpu.VMEM(half, F32), pltpu.VMEM((4, *half), F32), pltpu.VMEM((3, *half), F32), pltpu.SemaphoreType.DMA((16 // OUT_CHUNK, 3))]

time: 59.9 us -> 59.9 us (level)
  transfers between devices with their start and end apart: 12 -> 12, of which waited for: 3 -> 3; matrix products, arithmetic and copies ran while one was open for 0% -> 0% of each run, Pallas kernels for 7% -> 8%
where the time goes in v4:
time: 59.9 us; the launch traced here: 59.6 us
  starting transfers between devices  31.3 us (52%)
  waiting for transfers between devices  17.5 us (29%)
  Pallas kernels  9.97 us (17%)
  between operations  0.85 us (1%)
    ppermute x12, starting transfers between devices, swap(): return lax.ppermute(x, axis, pairs)  31.3 us
    ppermute x12, waiting for transfers between devices, swap(): return lax.ppermute(x, axis, pairs)  17.5 us
    pallas_call x6, Pallas kernels, call(): pl.pallas_call(kernel, out_shape=[jax.ShapeDtypeStruct(out[0], out[2] if...  9.97 us
  transfers between devices with their start and end apart: 12, of which 3 were waited for; matrix products, arithmetic and copies ran while one was open for 0% of the time, Pallas kernels for 8%

profile of v4, /device:TPU:56, one launch (start us, length us, event | category | flops | bytes accessed | tf_op | source)
XLA Modules:
  0.0 59.6 jit_solution(4279860831740251189)
XLA Ops:
  0.7 2.9 %shard_map.93 = (f32[2,16,16,128]{3,2,1,0:T(8,128)S(1)}, f32[2,16,16,128]{3,2,1,0:T(8,128)S(1)}, f32[16,128]{1,0:T(8,128)S(1)}, f32[16,128]{1,0:T(8,128)S(1)}, f...) custom-call(f32[2,16,16,128]{3,2,1,0:T(8,128)} %cot_h.1, ...), custom_call_target="tpu_custom_call" | custom-call | flops 2621440 | bytes 4194304 | tf_op jit(solution)/shard_map/pallas_call | solution.py:393
  3.6 1.6 %collective-permute-start.2 = (f32[2,16,16,128]{3,2,1,0:T(8,128)S(1)}, f32[2,16,16,128]{3,2,1,0:T(8,128)S(1)}, u32[]{:S(2)}, u32[]{:S(2)}) collective-permute-start(f32[2,16,16,128]{3,2,1,0:T(8,128)S(1)} %get-tuple-element.65), channel_id=1, source_target_pairs={{0,4},{4,0},{8,12},{12,8},{16,20},{20,16},{24,28},{28,24},{32,36},... | collective-permute-start | bytes 786440 | tf_op jit(solution)/shard_map/ppermute | solution.py:409
  5.1 9.0 %collective-permute-start.3 = (f32[2,16,16,128]{3,2,1,0:T(8,128)S(1)}, f32[2,16,16,128]{3,2,1,0:T(8,128)S(1)}, u32[]{:S(2)}, u32[]{:S(2)}) collective-permute-start(f32[2,16,16,128]{3,2,1,0:T(8,128)S(1)} %get-tuple-element.66), channel_id=1, source_target_pairs={{4,8},{8,4},{12,16},{16,12},{20,24},{24,20},{28,32},{32,28},{36,40... | collective-permute-start | bytes 786440 | tf_op jit(solution)/shard_map/ppermute | solution.py:409
  14.2 0.1 collective-permute-start
  14.3 3.0 %collective-permute-start.1 = (f32[16,128]{1,0:T(8,128)S(1)}, f32[16,128]{1,0:T(8,128)S(1)}, u32[]{:S(2)}, u32[]{:S(2)}) collective-permute-start(f32[16,128]{1,0:T(8,128)S(1)} %get-tuple-element.54), channel_id=1, source_target_pairs={{1,2},{2,1},{5,6},{6,5},{9,10},{10,9},{13,14},{14,13},{17,18},{18,... | collective-permute-start | bytes 24584 | tf_op jit(solution)/shard_map/ppermute | solution.py:409
  17.3 0.0 collective-permute-done.r1
  17.3 6.5 %collective-permute-done.1.r2 = f32[16,128]{1,0:T(8,128)S(1)} collective-permute-done((f32[16,128]{1,0:T(8,128)S(1)}, f32[16,128]{1,0:T(8,128)S(1)}, u32[]{:S(2)}, u32[]{:S(2)}) %collective-permute-start.1) | collective-permute-done | bytes 8224 | tf_op jit(solution)/shard_map/ppermute | solution.py:409
  23.8 1.9 %collective-permute-start.5 = (f32[2,16,128]{2,1,0:T(8,128)S(1)}, f32[2,16,128]{2,1,0:T(8,128)S(1)}, u32[]{:S(2)}, u32[]{:S(2)}) collective-permute-start(f32[2,16,128]{2,1,0:T(8,128)S(1)} %pad_maximum_fusion), channel_id=1, source_target_pairs={{4,8},{8,4},{12,16},{16,12},{20,24},{24,20},{28,32},{32,28},{36,40... | collective-permute-start | bytes 49160 | tf_op jit(solution)/shard_map/ppermute | solution.py:409
  25.7 0.1 collective-permute-start.4
  25.8 0.0 copy-start.2
  25.8 0.7 %shard_map.94 = (f32[2,16,16,128]{3,2,1,0:T(8,128)S(1)}, f32[2,16,16,128]{3,2,1,0:T(8,128)S(1)}) custom-call(f32[2,16,16,128]{3,2,1,0:T(8,128)S(1)} %get-tuple-element.51.val, f32[4,2,16,16,128]{4,3,2,1,0:T(8,128)S(1)} %copy-done.1, f32[6,2,16,16,128]{4,3,2,1,0:T(8,128)S(1)} %copy-done, f32[16,128]{1,0:T(8,128)S(1)} %collective-permute-done.r1, ...), custom_call_target="tpu_custom_call" | custom-call | flops 2621440 | bytes 4194304 | tf_op jit(solution)/shard_map/pallas_call | solution.py:393
  26.6 8.0 %collective-permute-done.5.cb = f32[2,16,128]{2,1,0:T(8,128)S(1)} collective-permute-done((f32[2,16,128]{2,1,0:T(8,128)S(1)}, f32[2,16,128]{2,1,0:T(8,128)S(1)}, u32[]{:S(2)}, u32[]{:S(2)}) %collective-permute-start.5) | collective-permute-done | bytes 16416 | tf_op jit(solution)/shard_map/ppermute | solution.py:409
  34.5 0.0 collective-permute-done.4.ca
  34.5 1.2 %shard_map.95 = (f32[2,16,16,128]{3,2,1,0:T(8,128)S(1)}, f32[2,16,16,128]{3,2,1,0:T(8,128)S(1)}, f32[16,128]{1,0:T(8,128)S(1)}, f32[16,128]{1,0:T(8,128)S(1)}, f...) custom-call(f32[2,16,16,128]{3,2,1,0:T(8,128)S(1)} %copy-done.2, ...), custom_call_target="tpu_custom_call" | custom-call | flops 3932160 | bytes 4194304 | tf_op jit(solution)/shard_map/pallas_call | solution.py:393
  35.7 0.1 collective-permute-start.10
  35.8 4.2 %collective-permute-start.8 = (f32[2,16,16,128]{3,2,1,0:T(8,128)S(1)}, f32[2,16,16,128]{3,2,1,0:T(8,128)S(1)}, u32[]{:S(2)}, u32[]{:S(2)}) collective-permute-start(f32[2,16,16,128]{3,2,1,0:T(8,128)S(1)} %get-tuple-element.84), channel_id=1, source_target_pairs={{4,8},{8,4},{12,16},{16,12},{20,24},{24,20},{28,32},{32,28},{36,40... | collective-permute-start | bytes 786440 | tf_op jit(solution)/shard_map/ppermute | solution.py:409
  40.1 0.1 collective-permute-start.6
  40.2 1.9 %collective-permute-start.7 = (f32[16,128]{1,0:T(8,128)S(1)}, f32[16,128]{1,0:T(8,128)S(1)}, u32[]{:S(2)}, u32[]{:S(2)}) collective-permute-start(f32[16,128]{1,0:T(8,128)S(1)} %get-tuple-element.72), channel_id=1, source_target_pairs={{1,2},{2,1},{5,6},{6,5},{9,10},{10,9},{13,14},{14,13},{17,18},{18,... | collective-permute-start | bytes 24584 | tf_op jit(solution)/shard_map/ppermute | solution.py:409
  42.1 0.0 collective-permute-done.6.s1
  42.1 3.0 %collective-permute-done.7.s2 = f32[16,128]{1,0:T(8,128)S(1)} collective-permute-done((f32[16,128]{1,0:T(8,128)S(1)}, f32[16,128]{1,0:T(8,128)S(1)}, u32[]{:S(2)}, u32[]{:S(2)}) %collective-permute-start.7) | collective-permute-done | bytes 8224 | tf_op jit(solution)/shard_map/ppermute | solution.py:409
  45.1 9.3 %collective-permute-start.9 = (f32[2,16,128]{2,1,0:T(8,128)S(1)}, f32[2,16,128]{2,1,0:T(8,128)S(1)}, u32[]{:S(2)}, u32[]{:S(2)}) collective-permute-start(f32[2,16,128]{2,1,0:T(8,128)S(1)} %pad_maximum_fusion.1), channel_id=1, source_target_pairs={{4,8},{8,4},{12,16},{16,12},{20,24},{24,20},{28,32},{32,28},{36,40... | collective-permute-start | bytes 49160 | tf_op jit(solution)/shard_map/ppermute | solution.py:409
  54.4 2.7 %shard_map.96 = (f32[2,16,16,128]{3,2,1,0:T(8,128)}, f32[6,2,16,16,128]{4,3,2,1,0:T(8,128)}, f32[2,16,16,128]{3,2,1,0:T(8,128)S(1)}, f32[4,2,16,16,128]{4,3,2,1,0:T(8,128)S(1)}, f32[3,2,16,16,128]{4,3,2,1,0:T(8,128)S(1)}) custom-call(f32[2,16,16,128]{3,2,1,0:T(8,128)S(1)} %get-tuple-element.51.val, f32[2,16,16,128]{3,2,1,0:T(8,128)S(1)} %get-tuple-element.67.u1, ...), custom_call_target="tpu_custom_call" | custom-call | flops 7864320 | bytes 4194304 | tf_op jit(solution)/shard_map/pallas_call | solution.py:393
  57.1 1.2 %shard_map.97 = (f32[2,16,16,128]{3,2,1,0:T(8,128)}, f32[4,2,16,16,128]{4,3,2,1,0:T(8,128)}, f32[6,2,16,16,128]{4,3,2,1,0:T(8,128)}) custom-call(f32[4,2,16,16,128]{4,3,2,1,0:T(8,128)S(1)} %copy-done.1, f32[6,2,16,16,128]{4,3,2,1,0:T(8,128)S(1)} %copy-done, f32[2,16,16,128]{3,2,1,0:T(8,128)S(1)} %get-tuple-element.49.inv, ...), custom_call_target="tpu_custom_call", output_to_operand_aliasing={{2}: (9, {})} | custom-call | flops 1310720 | bytes 4194304 | tf_op jit(solution)/shard_map/pallas_call | solution.py:393
  58.4 1.2 %shard_map.98 = (f32[2,16,16,128]{3,2,1,0:T(8,128)}, f32[4,2,16,16,128]{4,3,2,1,0:T(8,128)}, f32[6,2,16,16,128]{4,3,2,1,0:T(8,128)}) custom-call(f32[4,2,16,16,128]{4,3,2,1,0:T(8,128)S(1)} %copy-done.1, f32[6,2,16,16,128]{4,3,2,1,0:T(8,128)S(1)} %copy-done, ...), custom_call_target="tpu_custom_call", output_to_operand_aliasing={{0}: (9, {}), {1}: (10, {}), {2}: (11, {})} | custom-call | flops 1310720 | bytes 4194304 | tf_op jit(solution)/shard_map/pallas_call | solution.py:393
  (14 shorter events, 0.0 us)
Async XLA Ops:
  0.6 25.2 %copy-start = (f32[6,2,16,16,128]{4,3,2,1,0:T(8,128)S(1)}, f32[6,2,16,16,128]{4,3,2,1,0:T(8,128)}, u32[]{:S(2)}) copy-start(f32[6,2,16,16,128]{4,3,2,1,0:T(8,128)} %crs.9) | copy-start | bytes 4718596
  0.6 25.2 %copy-start.1 = (f32[4,2,16,16,128]{4,3,2,1,0:T(8,128)S(1)}, f32[4,2,16,16,128]{4,3,2,1,0:T(8,128)}, u32[]{:S(2)}) copy-start(f32[4,2,16,16,128]{4,3,2,1,0:T(8,128)} %dif.9) | copy-start | bytes 3145732
  3.6 31.0 %collective-permute-start.2 = (f32[2,16,16,128]{3,2,1,0:T(8,128)S(1)}, f32[2,16,16,128]{3,2,1,0:T(8,128)S(1)}, u32[]{:S(2)}, u32[]{:S(2)}) collective-permute-start(f32[2,16,16,128]{3,2,1,0:T(8,128)S(1)} %get-tuple-element.65), channel_id=1, source_target_pairs={{0,4},{4,0},{8,12},{12,8},{16,20},{20,16},{24,28},{28,24},{32,36},... | collective-permute-start | bytes 786440 | tf_op jit(solution)/shard_map/ppermute | solution.py:409
  5.1 29.4 %collective-permute-start.3 = (f32[2,16,16,128]{3,2,1,0:T(8,128)S(1)}, f32[2,16,16,128]{3,2,1,0:T(8,128)S(1)}, u32[]{:S(2)}, u32[]{:S(2)}) collective-permute-start(f32[2,16,16,128]{3,2,1,0:T(8,128)S(1)} %get-tuple-element.66), channel_id=1, source_target_pairs={{4,8},{8,4},{12,16},{16,12},{20,24},{24,20},{28,32},{32,28},{36,40... | collective-permute-start | bytes 786440 | tf_op jit(solution)/shard_map/ppermute | solution.py:409
  14.2 3.1 %collective-permute-start = (f32[16,128]{1,0:T(8,128)S(1)}, f32[16,128]{1,0:T(8,128)S(1)}, u32[]{:S(2)}, u32[]{:S(2)}) collective-permute-start(f32[16,128]{1,0:T(8,128)S(1)} %get-tuple-element.53), channel_id=1, source_target_pairs={{0,1},{1,0},{2,3},{3,2},{4,5},{5,4},{6,7},{7,6},{8,9},{9,8},{10,11... | collective-permute-start | bytes 24584 | tf_op jit(solution)/shard_map/ppermute | solution.py:409
  14.3 9.5 %collective-permute-start.1 = (f32[16,128]{1,0:T(8,128)S(1)}, f32[16,128]{1,0:T(8,128)S(1)}, u32[]{:S(2)}, u32[]{:S(2)}) collective-permute-start(f32[16,128]{1,0:T(8,128)S(1)} %get-tuple-element.54), channel_id=1, source_target_pairs={{1,2},{2,1},{5,6},{6,5},{9,10},{10,9},{13,14},{14,13},{17,18},{18,... | collective-permute-start | bytes 24584 | tf_op jit(solution)/shard_map/ppermute | solution.py:409
  23.8 10.7 %collective-permute-start.5 = (f32[2,16,128]{2,1,0:T(8,128)S(1)}, f32[2,16,128]{2,1,0:T(8,128)S(1)}, u32[]{:S(2)}, u32[]{:S(2)}) collective-permute-start(f32[2,16,128]{2,1,0:T(8,128)S(1)} %pad_maximum_fusion), channel_id=1, source_target_pairs={{4,8},{8,4},{12,16},{16,12},{20,24},{24,20},{28,32},{32,28},{36,40... | collective-permute-start | bytes 49160 | tf_op jit(solution)/shard_map/ppermute | solution.py:409
  25.7 8.8 %collective-permute-start.4 = (f32[2,16,128]{2,1,0:T(8,128)S(1)}, f32[2,16,128]{2,1,0:T(8,128)S(1)}, u32[]{:S(2)}, u32[]{:S(2)}) collective-permute-start(f32[2,16,128]{2,1,0:T(8,128)S(1)} %pad_maximum_fusion), channel_id=1, source_target_pairs={{0,4},{4,0},{8,12},{12,8},{16,20},{20,16},{24,28},{28,24},{32,36},... | collective-permute-start | bytes 49160 | tf_op jit(solution)/shard_map/ppermute | solution.py:409
  25.8 8.7 %copy-start.2 = (f32[2,16,16,128]{3,2,1,0:T(8,128)S(1)}, f32[2,16,16,128]{3,2,1,0:T(8,128)}, u32[]{:S(2)}) copy-start(f32[2,16,16,128]{3,2,1,0:T(8,128)} %pay.1) | copy-start | bytes 786436
  35.7 21.4 %collective-permute-start.10 = (f32[2,16,16,128]{3,2,1,0:T(8,128)S(1)}, f32[2,16,16,128]{3,2,1,0:T(8,128)S(1)}, u32[]{:S(2)}, u32[]{:S(2)}) collective-permute-start(f32[2,16,16,128]{3,2,1,0:T(8,128)S(1)} %get-tuple-element.85), channel_id=1, source_target_pairs={{0,4},{4,0},{8,12},{12,8},{16,20},{20,16},{24,28},{28,24},{32,36},... | collective-permute-start | bytes 786440 | tf_op jit(solution)/shard_map/ppermute | solution.py:409
  35.8 22.5 %collective-permute-start.8 = (f32[2,16,16,128]{3,2,1,0:T(8,128)S(1)}, f32[2,16,16,128]{3,2,1,0:T(8,128)S(1)}, u32[]{:S(2)}, u32[]{:S(2)}) collective-permute-start(f32[2,16,16,128]{3,2,1,0:T(8,128)S(1)} %get-tuple-element.84), channel_id=1, source_target_pairs={{4,8},{8,4},{12,16},{16,12},{20,24},{24,20},{28,32},{32,28},{36,40... | collective-permute-start | bytes 786440 | tf_op jit(solution)/shard_map/ppermute | solution.py:409
  40.1 2.0 %collective-permute-start.6 = (f32[16,128]{1,0:T(8,128)S(1)}, f32[16,128]{1,0:T(8,128)S(1)}, u32[]{:S(2)}, u32[]{:S(2)}) collective-permute-start(f32[16,128]{1,0:T(8,128)S(1)} %get-tuple-element.71), channel_id=1, source_target_pairs={{0,1},{1,0},{2,3},{3,2},{4,5},{5,4},{6,7},{7,6},{8,9},{9,8},{10,11... | collective-permute-start | bytes 24584 | tf_op jit(solution)/shard_map/ppermute | solution.py:409
  40.2 5.0 %collective-permute-start.7 = (f32[16,128]{1,0:T(8,128)S(1)}, f32[16,128]{1,0:T(8,128)S(1)}, u32[]{:S(2)}, u32[]{:S(2)}) collective-permute-start(f32[16,128]{1,0:T(8,128)S(1)} %get-tuple-element.72), channel_id=1, source_target_pairs={{1,2},{2,1},{5,6},{6,5},{9,10},{10,9},{13,14},{14,13},{17,18},{18,... | collective-permute-start | bytes 24584 | tf_op jit(solution)/shard_map/ppermute | solution.py:409
  45.1 12.0 %collective-permute-start.11 = (f32[2,16,128]{2,1,0:T(8,128)S(1)}, f32[2,16,128]{2,1,0:T(8,128)S(1)}, u32[]{:S(2)}, u32[]{:S(2)}) collective-permute-start(f32[2,16,128]{2,1,0:T(8,128)S(1)} %pad_maximum_fusion.1), channel_id=1, source_target_pairs={{0,4},{4,0},{8,12},{12,8},{16,20},{20,16},{24,28},{28,24},{32,36},... | collective-permute-start | bytes 49160 | tf_op jit(solution)/shard_map/ppermute | solution.py:409
  45.1 13.2 %collective-permute-start.9 = (f32[2,16,128]{2,1,0:T(8,128)S(1)}, f32[2,16,128]{2,1,0:T(8,128)S(1)}, u32[]{:S(2)}, u32[]{:S(2)}) collective-permute-start(f32[2,16,128]{2,1,0:T(8,128)S(1)} %pad_maximum_fusion.1), channel_id=1, source_target_pairs={{4,8},{8,4},{12,16},{16,12},{20,24},{24,20},{28,32},{32,28},{36,40... | collective-permute-start | bytes 49160 | tf_op jit(solution)/shard_map/ppermute | solution.py:409
